TPU v7x, 32 devices: a 4x4x1 block of a 4x4x8 slice. The times are simulated.
32 devices in a mesh: rep: 2 (over z, core), dp: 16 (over x, y).
Axes of the slice: x: 4, y: 4, z: 1, core: 2. Of those that a mesh axis runs over, the one named last changes fastest.
The devices are a block of a 4x4x8 slice.
Arguments:
- x: bfloat16 [32, 4096, 512], P(('rep', 'dp')), parts along dimension 0
- dy: bfloat16 [32, 4096, 512], P(('rep', 'dp')), parts along dimension 0
- w_gate: bfloat16 [2, 512, 2048], P(None, 'dp')
- w_up: bfloat16 [2, 512, 2048], P(None, 'dp')
- w_down: bfloat16 [2, 2048, 512], P(None, 'dp')
- m_w_gate: float32 [2, 512, 2048], P(None, 'dp')
- m_w_up: float32 [2, 512, 2048], P(None, 'dp')
- m_w_down: float32 [2, 2048, 512], P(None, 'dp')
- v_w_gate: float32 [2, 512, 2048], P(None, 'dp')
- v_w_up: float32 [2, 512, 2048], P(None, 'dp')
- v_w_down: float32 [2, 2048, 512], P(None, 'dp')
Outputs:
- output 1: bfloat16 [4, 512, 2048], P('rep', 'dp'), parts along dimension 0
- output 2: bfloat16 [4, 512, 2048], P('rep', 'dp'), parts along dimension 0
- output 3: bfloat16 [4, 2048, 512], P('rep', 'dp'), parts along dimension 0
- output 4: float32 [4, 512, 2048], P('rep', 'dp'), parts along dimension 0
- output 5: float32 [4, 512, 2048], P('rep', 'dp'), parts along dimension 0
- output 6: float32 [4, 2048, 512], P('rep', 'dp'), parts along dimension 0
- output 7: float32 [4, 512, 2048], P('rep', 'dp'), parts along dimension 0
- output 8: float32 [4, 512, 2048], P('rep', 'dp'), parts along dimension 0
- output 9: float32 [4, 2048, 512], P('rep', 'dp'), parts along dimension 0
There are 2 independent parts. A program takes and returns all parts, laid end to end along the dimension named above; an argument that names none is the same for every part.
All inputs are finite; a program needn't handle non-finite values.
Results may differ from a plain program's by a relative error of at most 0.02.
Values are sent between devices in bfloat16 or wider.
A program may use at most 768 MiB of HBM per device.

v0:
```python
import jax
import jax.numpy as jnp
from jax import lax
from jax.sharding import PartitionSpec as P

NAMES = ("w_gate", "w_up", "w_down")


def matmul(a, w):
    return jnp.dot(a, w, preferred_element_type=jnp.float32).astype(jnp.bfloat16)


def normed(h):
    wide = h.astype(jnp.float32)
    scale = lax.rsqrt(jnp.mean(wide**2, -1, keepdims=True) + 1e-6)
    return (wide * scale).astype(jnp.bfloat16)


def layer(h, w):
    a = normed(h)
    gate = jnp.dot(a, w["w_gate"], preferred_element_type=jnp.float32)
    up = jnp.dot(a, w["w_up"], preferred_element_type=jnp.float32)
    return h + matmul((jax.nn.silu(gate) * up).astype(jnp.bfloat16), w["w_down"])


def adamw(w, m, v, g):
    m = 0.9 * m + 0.1 * g
    v = 0.95 * v + 0.05 * g * g
    step = m * lax.rsqrt(v + 1e-8) + 0.1 * w
    return (w - 0.02 * step).astype(jnp.bfloat16), m, v


def solution(mesh):
    def fetched(weights, number):
        return {name: lax.all_gather(w[number], "dp", axis=0, tiled=True) for name, w in zip(NAMES, weights, strict=True)}

    def step(x, dy, *arrays):
        weights, m, v = (arrays[i : i + 3] for i in (0, 3, 6))
        layers = weights[0].shape[0]
        h, kept = x[0], []
        for number in range(layers):
            kept.append(h)
            h = layer(h, fetched(weights, number))
        by_h, mine = dy[0], [None] * layers
        for number in reversed(range(layers)):
            _, back = jax.vjp(lambda w, h: layer(h, w), fetched(weights, number), kept[number])
            by_w, by_h = back(by_h)
            mine[number] = [lax.psum_scatter(by_w[name], "dp", scatter_dimension=0, tiled=True) for name in NAMES]
        gradients = [jnp.stack([mine[number][i] for number in range(layers)]).astype(jnp.float32) for i in range(3)]
        new = [adamw(w.astype(jnp.float32), m, v, g) for w, m, v, g in zip(weights, m, v, gradients, strict=True)]
        return tuple(one[which] for which in range(3) for one in new)

    states, cut = P(("rep", "dp"), None, None), P(None, "dp", None)
    return jax.shard_map(
        step,
        mesh=mesh,
        in_specs=(states, states) + (cut,) * 9,
        out_specs=(P("rep", "dp", None),) * 9,
        check_vma=False,
    )
```

profile of v0, /device:TPU:97, one launch (start us, length us, event | category | flops | bytes accessed | tf_op | source)
XLA Modules:
  0.0 799.5 jit_solution(840827631853814218)
XLA Ops:
  7.2 0.1 all-gather.13.cloned.1.call-start
  7.3 1.7 fusion.87
  8.9 0.1 all-gather.13.cloned.1.call-update
  9.0 0.1 all-gather.15.cloned.1.call-start
  9.1 1.7 fusion.86
  10.8 0.1 all-gather.15.cloned.1.call-update
  10.8 0.1 all-gather.17.cloned.1.call-start
  10.9 1.7 fusion.85
  12.6 0.1 all-gather.17.cloned.1.call-update
  12.6 0.1 all-gather.21.cloned.1.call-start
  12.7 0.6 all-gather.21.cloned.1.call-update
  13.3 0.1 all-gather.23.cloned.1.call-start
  13.4 0.6 all-gather.23.cloned.1.call-update
  13.9 0.1 all-gather.19.cloned.1.call-start
  14.0 0.6 all-gather.19.cloned.1.call-update
  14.6 0.1 reduce-scatter.15.cloned.1.call-start
  14.6 6.4 copy.20
  21.1 3.1 fusion.15
  24.2 6.4 copy.21
  30.6 21.9 %all-gather.13.cloned.1.call-done = bf16[1,512,2048]{2,1,0:T(8,128)(2,1)} async-done(((bf16[1,32,2048]{2,1,0:T(8,128)(2,1)}), bf16[1,512,2048]{2,1,0:T(8,128)(2,1)}) %all-gather.13.cloned.1.call-update) | async-done | bytes 2097168 | tf_op jit(solution)/shard_map/all_gather | solution.py:35
  52.4 17.8 %fusion.47 = f32[4096,2048]{1,0:T(8,128)} fusion(bf16[1,4096,512]{1,2,0:T(8,128)(2,1)} %copy.20, f32[4096]{0:T(1024)S(1)} %add_rsqrt_fusion, bf16[1,512,2048]{2,1,0:T(8,128)(2,1)} %all-gather.13.cloned.1.call-done), kind=kOutput, calls=%fused_computation.57 | convolution fusion | flops 8596226048 | bytes 39862272 | tf_op jit(solution)/shard_map/dot_general | solution.py:21
  70.3 23.8 %all-gather.15.cloned.1.call-done = bf16[1,512,2048]{2,1,0:T(8,128)(2,1)} async-done(((bf16[1,32,2048]{2,1,0:T(8,128)(2,1)}), bf16[1,512,2048]{2,1,0:T(8,128)(2,1)}) %all-gather.15.cloned.1.call-update) | async-done | bytes 2097168 | tf_op jit(solution)/shard_map/all_gather | solution.py:35
  94.0 31.4 %multiply_convert_fusion.1 = (bf16[4096,2048]{1,0:T(8,128)(2,1)}, f32[4096,2048]{1,0:T(8,128)}) fusion(f32[4096,2048]{1,0:T(8,128)} %fusion.47, bf16[1,512,2048]{2,1,0:T(8,128)(2,1)} %all-gather.15.cloned.1.call-done, bf16[1,4096,512]{1,2,0:T(8,128)(2,1)} %copy.20, f32[4096]{0:T(1024)S(1)} %add_rsqrt_fusion), kind=kOutput, calls=%fused_computation.17 | convolution fusion | flops 8646557696 | bytes 90193920 | tf_op jit(solution)/shard_map/dot_general | solution.py:22
  125.4 10.2 %all-gather.17.cloned.1.call-done = bf16[1,2048,512]{2,1,0:T(8,128)(2,1)} async-done(((bf16[1,128,512]{2,1,0:T(8,128)(2,1)}), bf16[1,2048,512]{2,1,0:T(8,128)(2,1)}) %all-gather.17.cloned.1.call-update) | async-done | bytes 2097168 | tf_op jit(solution)/shard_map/all_gather | solution.py:35
  135.6 16.0 %fusion.19 = (f32[4096]{0:T(1024)S(1)}, bf16[4096,512]{0,1:T(8,128)(2,1)}) fusion(bf16[4096,2048]{1,0:T(8,128)(2,1)} %get-tuple-element.24, bf16[1,2048,512]{2,1,0:T(8,128)(2,1)} %all-gather.17.cloned.1.call-done, bf16[1,4096,512]{1,2,0:T(8,128)(2,1)} %copy.20), kind=kOutput, calls=%fused_computation.37 | convolution fusion | flops 8600416256 | bytes 27279360 | tf_op jit(solution)/shard_map/dot_general | solution.py:10
  151.7 25.4 %all-gather.21.cloned.1.call-done = bf16[1,2048,512]{2,1,0:T(8,128)(2,1)} async-done(((bf16[1,128,512]{2,1,0:T(8,128)(2,1)}), bf16[1,2048,512]{2,1,0:T(8,128)(2,1)}) %all-gather.21.cloned.1.call-update) | async-done | bytes 2097168 | tf_op jit(solution)/shard_map/all_gather | solution.py:35
  177.1 14.9 %convolution_convert_fusion.1 = bf16[4096,2048]{1,0:T(8,128)(2,1)} fusion(bf16[1,4096,512]{2,1,0:T(8,128)(2,1)} %param.12, bf16[1,2048,512]{2,1,0:T(8,128)(2,1)} %all-gather.21.cloned.1.call-done), kind=kOutput, calls=%fused_computation.25 | convolution fusion | flops 8598323200 | bytes 23068672 | tf_op jit(solution)/shard_map/transpose(jvp())/dot_general | solution.py:10
  192.0 26.5 %all-gather.23.cloned.1.call-done = bf16[1,512,2048]{2,1,0:T(8,128)(2,1)} async-done(((bf16[1,32,2048]{2,1,0:T(8,128)(2,1)}), bf16[1,512,2048]{2,1,0:T(8,128)(2,1)}) %all-gather.23.cloned.1.call-update) | async-done | bytes 2097168 | tf_op jit(solution)/shard_map/all_gather | solution.py:35
  218.5 18.0 %fusion.39 = f32[4096,2048]{1,0:T(8,128)} fusion(bf16[4096,512]{0,1:T(8,128)(2,1)} %get-tuple-element.27, f32[4096]{0:T(1024)S(1)} %fusion.73, bf16[1,512,2048]{2,1,0:T(8,128)(2,1)} %all-gather.23.cloned.1.call-done), kind=kOutput, calls=%fused_computation.54 | convolution fusion | flops 8596226048 | bytes 39862272 | tf_op jit(solution)/shard_map/jvp()/dot_general | solution.py:22
  236.6 23.4 %all-gather.19.cloned.1.call-done = bf16[1,512,2048]{2,1,0:T(8,128)(2,1)} async-done(((bf16[1,32,2048]{2,1,0:T(8,128)(2,1)}), bf16[1,512,2048]{2,1,0:T(8,128)(2,1)}) %all-gather.19.cloned.1.call-update) | async-done | bytes 2097168 | tf_op jit(solution)/shard_map/all_gather | solution.py:35
  260.0 41.1 %fusion.2 = (bf16[4096,2048]{1,0:T(8,128)(2,1)}, f32[4096,2048]{1,0:T(8,128)}) fusion(f32[4096,2048]{1,0:T(8,128)} %fusion.39, bf16[4096,2048]{1,0:T(8,128)(2,1)} %convolution_convert_fusion.1, bf16[1,512,2048]{2,1,0:T(8,128)(2,1)} %all-gather.19.cloned.1.call-done, bf16[4096,512]{0,1:T(8,128)(2,1)} %get-tuple-element.27, f32[4096]{0:T(1024)S(1)} %fusion.73), kind=kOutput, calls=%fused_computation.8 | convolution fusion | flops 8696889344 | bytes 106971136 | tf_op jit(solution)/shard_map/jvp()/dot_general | solution.py:21
  301.1 21.8 %fusion.22 = bf16[4096,512]{0,1:T(8,128)(2,1)} fusion(bf16[4096,2048]{1,0:T(8,128)(2,1)} %convolution_convert_fusion.1, bf16[1,512,2048]{2,1,0:T(8,128)(2,1)S(1)} %copy-done.19, f32[4096,2048]{1,0:T(8,128)} %get-tuple-element.29), kind=kOutput, calls=%fused_computation.40 | convolution fusion | flops 8642363392 | bytes 56623104 | tf_op jit(solution)/shard_map/transpose(jvp())/dot_general | solution.py:22
  322.9 16.8 %fusion.21 = (f32[4096]{0:T(1024)S(1)}, bf16[4096,512]{0,1:T(8,128)(2,1)S(1)}) fusion(bf16[4096,512]{0,1:T(8,128)(2,1)S(1)} %copy-done.2, bf16[4096,512]{0,1:T(8,128)(2,1)} %fusion.22, bf16[4096,2048]{1,0:T(8,128)(2,1)} %get-tuple-element.28, bf16[1,512,2048]{2,1,0:T(8,128)(2,1)} %all-gather.19.cloned.1.call-done), kind=kOutput, calls=%fused_computation.39 | convolution fusion | flops 8600416256 | bytes 31473664 | tf_op jit(solution)/shard_map/transpose(jvp())/dot_general | solution.py:21
  339.7 2.8 fusion.26
  342.6 2.0 copy-done.3
  344.6 14.0 %convolution_convert_fusion.4 = bf16[2048,512]{1,0:T(8,128)(2,1)} fusion(bf16[4096,2048]{1,0:T(8,128)(2,1)} %get-tuple-element.24, bf16[4096,512]{0,1:T(8,128)(2,1)S(1)} %fusion.26), kind=kOutput, calls=%fused_computation.50 | convolution fusion | flops 8590983168 | bytes 23068672 | tf_op jit(solution)/shard_map/transpose(jvp())/dot_general | solution.py:10
  358.6 0.1 reduce-scatter.15.cloned.1.call-update
  358.6 0.1 reduce-scatter.17.cloned.1.call-start
  358.7 25.5 %fusion.30 = bf16[2048,512]{1,0:T(8,128)(2,1)} fusion(bf16[1,4096,512]{2,1,0:T(8,128)(2,1)} %param.12, f32[4096,2048]{1,0:T(8,128)} %fusion.39, f32[4096,2048]{1,0:T(8,128)} %get-tuple-element.29), kind=kOutput, calls=%fused_computation.49 | convolution fusion | flops 8641314816 | bytes 73400320 | tf_op jit(solution)/shard_map/transpose(jvp())/dot_general | solution.py:10
  384.2 0.1 reduce-scatter.17.cloned.1.call-update
  384.3 0.0 copy-start.17
  384.3 0.1 reduce-scatter.11.cloned.1.call-start
  384.4 15.0 %convolution_convert_fusion = bf16[4096,2048]{1,0:T(8,128)(2,1)} fusion(bf16[4096,512]{0,1:T(8,128)(2,1)} %copy-done.3, bf16[1,2048,512]{2,1,0:T(8,128)(2,1)S(1)} %copy-done.18), kind=kOutput, calls=%fused_computation.24 | convolution fusion | flops 8598323200 | bytes 23068672 | tf_op jit(solution)/shard_map/transpose(jvp())/dot_general | solution.py:10
  399.4 20.6 %fusion.36 = bf16[512,2048]{1,0:T(8,128)(2,1)} fusion(bf16[4096,2048]{1,0:T(8,128)(2,1)} %convolution_convert_fusion, f32[4096,2048]{1,0:T(8,128)} %fusion.47, bf16[1,4096,512]{1,2,0:T(8,128)(2,1)S(1)} %copy-done, f32[4096]{0:T(1024)S(1)} %copy-done.17), kind=kOutput, calls=%fused_computation.53 | convolution fusion | flops 8647606272 | bytes 56639488 | tf_op jit(solution)/shard_map/transpose(jvp())/dot_general | solution.py:22
  420.0 0.1 reduce-scatter.11.cloned.1.call-update
  420.1 0.1 reduce-scatter.13.cloned.1.call-start
  420.2 22.4 %fusion.29 = bf16[512,2048]{1,0:T(8,128)(2,1)} fusion(bf16[4096,2048]{1,0:T(8,128)(2,1)} %convolution_convert_fusion.1, bf16[4096,512]{0,1:T(8,128)(2,1)} %get-tuple-element.27, f32[4096]{0:T(1024)S(1)} %copy-done.15, f32[4096,2048]{1,0:T(8,128)} %get-tuple-element.29), kind=kOutput, calls=%fused_computation.48 | convolution fusion | flops 8647606272 | bytes 56639488 | tf_op jit(solution)/shard_map/transpose(jvp())/dot_general | solution.py:22
  442.6 0.1 reduce-scatter.13.cloned.1.call-update
  442.6 0.1 reduce-scatter.7.cloned.1.call-start
  442.7 34.3 %fusion.33 = bf16[512,2048]{1,0:T(8,128)(2,1)} fusion(f32[4096,2048]{1,0:T(8,128)} %fusion.47, f32[4096,2048]{1,0:T(8,128)} %get-tuple-element.25, bf16[4096,2048]{1,0:T(8,128)(2,1)} %convolution_convert_fusion, bf16[1,4096,512]{1,2,0:T(8,128)(2,1)} %copy.20, f32[4096]{0:T(1024)S(1)} %copy-done.17), kind=kOutput, calls=%fused_computation.52 | convolution fusion | flops 8689549312 | bytes 90193920 | tf_op jit(solution)/shard_map/transpose(jvp())/dot_general | solution.py:21
  477.0 0.1 reduce-scatter.7.cloned.1.call-update
  477.1 0.0 copy-start.4
  477.2 0.1 reduce-scatter.9.cloned.1.call-start
  477.2 14.7 %convolution_convert_fusion.5 = bf16[512,2048]{1,0:T(8,128)(2,1)} fusion(bf16[4096,2048]{1,0:T(8,128)(2,1)} %get-tuple-element.28, bf16[4096,512]{0,1:T(8,128)(2,1)} %get-tuple-element.27, f32[4096]{0:T(1024)S(1)} %copy-done.15), kind=kOutput, calls=%fused_computation.51 | convolution fusion | flops 8596226048 | bytes 23085056 | tf_op jit(solution)/shard_map/transpose(jvp())/dot_general | solution.py:21
  492.0 0.1 reduce-scatter.9.cloned.1.call-update
  492.0 0.0 reduce-scatter.15.cloned.1.call-done
  492.1 8.5 %reduce-scatter.17.cloned.1.call-done = bf16[128,512]{1,0:T(8,128)(2,1)} async-done(((bf16[2048,512]{1,0:T(8,128)(2,1)}), bf16[128,512]{1,0:T(8,128)(2,1)}) %reduce-scatter.17.cloned.1.call-update) | async-done | bytes 131088 | tf_op jit(solution)/shard_map/reduce_scatter | solution.py:48
  500.6 2.2 fusion.68
  502.8 70.3 %reduce-scatter.11.cloned.1.call-done = bf16[32,2048]{1,0:T(8,128)(2,1)} async-done(((bf16[512,2048]{1,0:T(8,128)(2,1)}), bf16[32,2048]{1,0:T(8,128)(2,1)}) %reduce-scatter.11.cloned.1.call-update) | async-done | bytes 131088 | tf_op jit(solution)/shard_map/reduce_scatter | solution.py:48
  573.0 72.3 %reduce-scatter.13.cloned.1.call-done = bf16[32,2048]{1,0:T(8,128)(2,1)} async-done(((bf16[512,2048]{1,0:T(8,128)(2,1)}), bf16[32,2048]{1,0:T(8,128)(2,1)}) %reduce-scatter.13.cloned.1.call-update) | async-done | bytes 131088 | tf_op jit(solution)/shard_map/reduce_scatter | solution.py:48
  645.3 2.1 fusion.64
  647.5 70.2 %reduce-scatter.7.cloned.1.call-done = bf16[32,2048]{1,0:T(8,128)(2,1)} async-done(((bf16[512,2048]{1,0:T(8,128)(2,1)}), bf16[32,2048]{1,0:T(8,128)(2,1)}) %reduce-scatter.7.cloned.1.call-update) | async-done | bytes 131088 | tf_op jit(solution)/shard_map/reduce_scatter | solution.py:48
  717.7 72.3 %reduce-scatter.9.cloned.1.call-done = bf16[32,2048]{1,0:T(8,128)(2,1)} async-done(((bf16[512,2048]{1,0:T(8,128)(2,1)}), bf16[32,2048]{1,0:T(8,128)(2,1)}) %reduce-scatter.9.cloned.1.call-update) | async-done | bytes 131088 | tf_op jit(solution)/shard_map/reduce_scatter | solution.py:48
  790.0 2.4 fusion.60
  (40 shorter events, 0.1 us)
Async XLA Ops:
  7.2 45.2 %all-gather.13.cloned.1.call-start = ((), (), s32[]{:S(2)}) async-start(), calls=%async_computation.12 | async-start | bytes 2228224 | tf_op jit(solution)/shard_map/all_gather | solution.py:35
  9.0 85.0 %all-gather.15.cloned.1.call-start = ((), (), s32[]{:S(2)}) async-start(), calls=%async_computation.13 | async-start | bytes 2228224 | tf_op jit(solution)/shard_map/all_gather | solution.py:35
  10.8 124.8 %all-gather.17.cloned.1.call-start = ((), (), s32[]{:S(2)}) async-start(), calls=%async_computation.14 | async-start | bytes 2228224 | tf_op jit(solution)/shard_map/all_gather | solution.py:35
  12.6 164.4 %all-gather.21.cloned.1.call-start = ((), (), s32[]{:S(2)}) async-start(), calls=%async_computation.16 | async-start | bytes 2228224 | tf_op jit(solution)/shard_map/all_gather | solution.py:35
  13.3 205.2 %all-gather.23.cloned.1.call-start = ((), (), s32[]{:S(2)}) async-start(), calls=%async_computation.17 | async-start | bytes 2228224 | tf_op jit(solution)/shard_map/all_gather | solution.py:35
  13.9 246.1 %all-gather.19.cloned.1.call-start = ((), (), s32[]{:S(2)}) async-start(), calls=%async_computation.15 | async-start | bytes 2228224 | tf_op jit(solution)/shard_map/all_gather | solution.py:35
  14.6 477.5 %reduce-scatter.15.cloned.1.call-start = ((), (), s32[]{:S(2)}) async-start(), calls=%async_computation.10 | async-start | bytes 2228224 | tf_op jit(solution)/shard_map/reduce_scatter | solution.py:48
  24.2 69.9 %copy-start.16 = (f32[4096]{0:T(1024)}, f32[4096]{0:T(1024)S(1)}, u32[]{:S(2)}) copy-start(f32[4096]{0:T(1024)S(1)} %add_rsqrt_fusion) | copy-start | bytes 49156
  151.6 40.4 %copy-start.12 = (f32[4096]{0:T(1024)}, f32[4096]{0:T(1024)S(1)}, u32[]{:S(2)}) copy-start(f32[4096]{0:T(1024)S(1)} %get-tuple-element.26) | copy-start | bytes 49156
  151.6 188.1 %copy-start.14 = (f32[4096]{0:T(1024)}, f32[4096]{0:T(1024)S(1)}, u32[]{:S(2)}) copy-start(f32[4096]{0:T(1024)S(1)} %fusion.73) | copy-start | bytes 49156
  236.6 64.5 %copy-start.19 = (bf16[1,512,2048]{2,1,0:T(8,128)(2,1)S(1)}, bf16[1,512,2048]{2,1,0:T(8,128)(2,1)}, u32[]{:S(2)}) copy-start(bf16[1,512,2048]{2,1,0:T(8,128)(2,1)} %all-gather.23.cloned.1.call-done) | copy-start | bytes 6291460
  301.1 21.8 %copy-start.2 = (bf16[4096,512]{0,1:T(8,128)(2,1)S(1)}, bf16[4096,512]{0,1:T(8,128)(2,1)}, u32[]{:S(2)}) copy-start(bf16[4096,512]{0,1:T(8,128)(2,1)} %get-tuple-element.27) | copy-start | bytes 12582916
  322.9 16.8 %copy-start.13 = (f32[4096]{0:T(1024)S(1)}, f32[4096]{0:T(1024)}, u32[]{:S(2)}) copy-start(f32[4096]{0:T(1024)} %copy-done.12) | copy-start | bytes 49156
  322.9 16.8 %copy-start.1 = (bf16[1,4096,512]{1,2,0:T(8,128)(2,1)S(1)}, bf16[1,4096,512]{1,2,0:T(8,128)(2,1)}, u32[]{:S(2)}) copy-start(bf16[1,4096,512]{1,2,0:T(8,128)(2,1)} %copy.21) | copy-start | bytes 12582916
  342.6 2.0 copy-start.3
  358.6 25.7 %copy-start.18 = (bf16[1,2048,512]{2,1,0:T(8,128)(2,1)S(1)}, bf16[1,2048,512]{2,1,0:T(8,128)(2,1)}, u32[]{:S(2)}) copy-start(bf16[1,2048,512]{2,1,0:T(8,128)(2,1)} %all-gather.17.cloned.1.call-done) | copy-start | bytes 6291460
  358.6 141.9 %reduce-scatter.17.cloned.1.call-start = ((), (), s32[]{:S(2)}) async-start(), calls=%async_computation.11 | async-start | bytes 2228224 | tf_op jit(solution)/shard_map/reduce_scatter | solution.py:48
  384.3 15.1 %copy-start.17 = (f32[4096]{0:T(1024)S(1)}, f32[4096]{0:T(1024)}, u32[]{:S(2)}) copy-start(f32[4096]{0:T(1024)} %copy-done.16) | copy-start | bytes 49156
  384.3 188.7 %reduce-scatter.11.cloned.1.call-start = ((), (), s32[]{:S(2)}) async-start(), calls=%async_computation.8 | async-start | bytes 2228224 | tf_op jit(solution)/shard_map/reduce_scatter | solution.py:48
  384.4 15.0 %copy-start = (bf16[1,4096,512]{1,2,0:T(8,128)(2,1)S(1)}, bf16[1,4096,512]{1,2,0:T(8,128)(2,1)}, u32[]{:S(2)}) copy-start(bf16[1,4096,512]{1,2,0:T(8,128)(2,1)} %copy.20) | copy-start | bytes 12582916
  399.4 20.8 %copy-start.15 = (f32[4096]{0:T(1024)S(1)}, f32[4096]{0:T(1024)}, u32[]{:S(2)}) copy-start(f32[4096]{0:T(1024)} %copy-done.14) | copy-start | bytes 49156
  420.1 225.2 %reduce-scatter.13.cloned.1.call-start = ((), (), s32[]{:S(2)}) async-start(), calls=%async_computation.9 | async-start | bytes 2228224 | tf_op jit(solution)/shard_map/reduce_scatter | solution.py:48
  442.6 275.1 %reduce-scatter.7.cloned.1.call-start = ((), (), s32[]{:S(2)}) async-start(), calls=%async_computation.6 | async-start | bytes 2228224 | tf_op jit(solution)/shard_map/reduce_scatter | solution.py:48
  477.1 23.5 %copy-start.4 = (bf16[2,128,512]{2,1,0:T(8,128)(2,1)S(1)}, bf16[2,128,512]{2,1,0:T(8,128)(2,1)}, u32[]{:S(2)}) copy-start(bf16[2,128,512]{2,1,0:T(8,128)(2,1)} %param.15) | copy-start | bytes 786436
  477.1 23.5 %copy-start.7 = (f32[2,128,512]{2,1,0:T(8,128)S(1)}, f32[2,128,512]{2,1,0:T(8,128)}, u32[]{:S(2)}) copy-start(f32[2,128,512]{2,1,0:T(8,128)} %param.21) | copy-start | bytes 1572868
  477.1 23.5 %copy-start.8 = (f32[2,128,512]{2,1,0:T(8,128)S(1)}, f32[2,128,512]{2,1,0:T(8,128)}, u32[]{:S(2)}) copy-start(f32[2,128,512]{2,1,0:T(8,128)} %param.18) | copy-start | bytes 1572868
  477.1 168.2 %copy-start.5 = (bf16[2,32,2048]{2,1,0:T(8,128)(2,1)S(1)}, bf16[2,32,2048]{2,1,0:T(8,128)(2,1)}, u32[]{:S(2)}) copy-start(bf16[2,32,2048]{2,1,0:T(8,128)(2,1)} %param.14) | copy-start | bytes 786436
  477.1 168.2 %copy-start.9 = (f32[2,32,2048]{2,1,0:T(8,128)S(1)}, f32[2,32,2048]{2,1,0:T(8,128)}, u32[]{:S(2)}) copy-start(f32[2,32,2048]{2,1,0:T(8,128)} %param.20) | copy-start | bytes 1572868
  477.1 168.2 %copy-start.10 = (f32[2,32,2048]{2,1,0:T(8,128)S(1)}, f32[2,32,2048]{2,1,0:T(8,128)}, u32[]{:S(2)}) copy-start(f32[2,32,2048]{2,1,0:T(8,128)} %param.17) | copy-start | bytes 1572868
  477.1 312.9 %copy-start.6 = (bf16[2,32,2048]{2,1,0:T(8,128)(2,1)S(1)}, bf16[2,32,2048]{2,1,0:T(8,128)(2,1)}, u32[]{:S(2)}) copy-start(bf16[2,32,2048]{2,1,0:T(8,128)(2,1)} %param.13) | copy-start | bytes 786436
  477.1 312.9 %copy-start.11 = (f32[2,32,2048]{2,1,0:T(8,128)S(1)}, f32[2,32,2048]{2,1,0:T(8,128)}, u32[]{:S(2)}) copy-start(f32[2,32,2048]{2,1,0:T(8,128)} %param.19) | copy-start | bytes 1572868
  477.2 312.8 %reduce-scatter.9.cloned.1.call-start = ((), (), s32[]{:S(2)}) async-start(), calls=%async_computation.7 | async-start | bytes 2228224 | tf_op jit(solution)/shard_map/reduce_scatter | solution.py:48
Sparse Core Ops, SparseCore 0:
  10.5 41.8 all-gather.12
  55.0 39.0 all-gather.14
  96.6 39.0 all-gather.16
  138.0 39.0 all-gather.20
  179.5 39.0 all-gather.22
  220.9 39.0 all-gather.18
  358.8 69.3 reduce-scatter.14
  431.3 69.2 reduce-scatter.16
  503.7 69.3 reduce-scatter.10
  576.0 69.3 reduce-scatter.12
  648.4 69.2 reduce-scatter.6
  720.6 69.3 reduce-scatter.8
where the time goes:
time: 808 us; the launch traced here: 799 us
  waiting for transfers between devices  427 us (53%)
  matrix products  324 us (40%)
  local copies, waits for them, and re-layouts  20 us (2%)
  between operations  14.7 us (2%)
  other arithmetic  12.6 us (2%)
    reduce_scatter x6, waiting for transfers between devices, step(): lax.psum_scatter(by_w[name], 'dp', scatter_dimension=0, tiled=True)  294 us
    all_gather x6, waiting for transfers between devices, fetched(): lax.all_gather(w[number], 'dp', axis=0, tiled=True)  131 us
    dot_general x5, matrix products, layer(): gate = jnp.dot(a, w['w_gate'], preferred_element_type=jnp.float32)  125 us
    dot_general x5, matrix products, layer(): up = jnp.dot(a, w['w_up'], preferred_element_type=jnp.float32)  114 us
    dot_general x5, matrix products, matmul(): jnp.dot(a, w, preferred_element_type=jnp.float32).astype(jnp.bfloat16)  85.5 us
  transfers between devices with their start and end apart: 12, of which 11 were waited for; matrix products, arithmetic and copies ran while one was open for 32% of the time, Pallas kernels for 0%

commit v1 on v0

v1 whole, which is shorter than its diff:
```python
import functools
import math

import jax, jax.numpy as jnp
from jax import lax
from jax.experimental import pallas as pl
from jax.experimental.pallas import tpu as pltpu
from jax.sharding import PartitionSpec as P

BF, F32 = jnp.bfloat16, jnp.float32
VM = 63 * 2**20

def dot(a, b, ca=1, cb=0):
    return lax.dot_general(a, b, (((ca,), (cb,)), ((), ())), preferred_element_type=F32)

def scale_of(wide):
    return lax.rsqrt(jnp.mean(wide * wide, -1, keepdims=True) + 1e-6)

def over(tokens, tile, unroll, body):
    def step(t, _):
        body(pl.ds(pl.multiple_of(t * tile, tile), tile))
        return 0
    lax.fori_loop(0, tokens // tile, step, 0, unroll=unroll)

def prepare(h_ref, a_ref, total):
    def first(rows):
        wide = h_ref[rows, :].astype(F32)
        a_ref[rows, :] = (wide * scale_of(wide)).astype(BF)
        if total is not None:
            total[rows, :] = jnp.zeros((rows.size, total.shape[1]), F32)
    over(h_ref.shape[0], 256, 1, first)

def forward_kernel(h_ref, wg_ref, wu_ref, wd_ref, out_ref, a_ref, total, *, chunks, tile, unroll):
    c = pl.program_id(0)
    pl.when(c == 0)(lambda: prepare(h_ref, a_ref, total))
    def main(rows):
        a = a_ref[rows, :]
        gate = dot(a, wg_ref[...])
        up = dot(a, wu_ref[...])
        act = (gate * jax.nn.sigmoid(gate) * up).astype(BF)
        total[rows, :] += dot(act, wd_ref[...])
    over(h_ref.shape[0], tile, unroll, main)
    @pl.when(c == chunks - 1)
    def _():
        def last(rows):
            out_ref[rows, :] = h_ref[rows, :] + total[rows, :].astype(BF)
        over(h_ref.shape[0], 256, 1, last)

def forward(h, wg, wu, wd, tile=512, chunk=512, unroll=1):
    tokens, d = h.shape; ff = wg.shape[1]
    chunks = ff // chunk
    tok = pl.BlockSpec((tokens, d), lambda c: (0, 0), pipeline_mode=pl.Buffered(1))
    col = pl.BlockSpec((d, chunk), lambda c: (0, c))
    return pl.pallas_call(
        functools.partial(forward_kernel, chunks=chunks, tile=tile, unroll=unroll),
        grid=(chunks,),
        in_specs=[tok, col, col, pl.BlockSpec((chunk, d), lambda c: (c, 0))],
        out_specs=tok,
        out_shape=jax.ShapeDtypeStruct(h.shape, BF),
        scratch_shapes=[pltpu.VMEM((tokens, d), BF), pltpu.VMEM((tokens, d), F32)],
        compiler_params=pltpu.CompilerParams(dimension_semantics=("arbitrary",), vmem_limit_bytes=VM),
        cost_estimate=pl.CostEstimate(flops=6 * tokens * d * ff, bytes_accessed=4 * tokens * d * chunks, transcendentals=tokens * ff),
        name="forward",
    )(h, wg, wu, wd)

def backward_kernel(h_ref, dy_ref, wg_ref, wu_ref, wd_ref, *rest, chunks, tile, unroll, carry):
    if carry:
        dh_ref, gg_ref, gu_ref, gd_ref, a_ref, sg, su, sd, total = rest
    else:
        gg_ref, gu_ref, gd_ref, a_ref, sg, su, sd = rest
        total = None
    c = pl.program_id(0)
    pl.when(c == 0)(lambda: prepare(h_ref, a_ref, total))
    sg[...] = jnp.zeros_like(sg); su[...] = jnp.zeros_like(su); sd[...] = jnp.zeros_like(sd)
    def main(rows):
        a, dy = a_ref[rows, :], dy_ref[rows, :]
        gate = dot(a, wg_ref[...])
        up = dot(a, wu_ref[...])
        dact = dot(dy, wd_ref[...], 1, 1).astype(BF).astype(F32)
        sig = jax.nn.sigmoid(gate)
        silu = gate * sig
        act = (silu * up).astype(BF)
        dup = (dact * silu).astype(BF)
        dgate = (dact * up * (sig + silu * (1 - sig))).astype(BF)
        sd[...] += dot(act, dy, 0, 0)
        sg[...] += dot(a, dgate, 0, 0)
        su[...] += dot(a, dup, 0, 0)
        if carry:
            total[rows, :] += dot(dgate, wg_ref[...], 1, 1) + dot(dup, wu_ref[...], 1, 1)
    over(h_ref.shape[0], tile, unroll, main)
    gd_ref[...] = sd[...].astype(BF); gg_ref[...] = sg[...].astype(BF); gu_ref[...] = su[...].astype(BF)
    if carry:
        @pl.when(c == chunks - 1)
        def _():
            def last(rows):
                wide = h_ref[rows, :].astype(F32)
                scale = scale_of(wide)
                da = total[rows, :].astype(BF).astype(F32)
                dwide = scale * (da - wide * (scale * scale * jnp.mean(da * wide, -1, keepdims=True)))
                dh_ref[rows, :] = dy_ref[rows, :] + dwide.astype(BF)
            over(h_ref.shape[0], 256, 1, last)

def backward(h, dy, wg, wu, wd, carry, tile=256, chunk=512, unroll=2):
    tokens, d = h.shape; ff = wg.shape[1]
    chunks = ff // chunk
    tok = pl.BlockSpec((tokens, d), lambda c: (0, 0), pipeline_mode=pl.Buffered(1))
    col = pl.BlockSpec((d, chunk), lambda c: (0, c))
    row = pl.BlockSpec((chunk, d), lambda c: (c, 0))
    outs = [jax.ShapeDtypeStruct(wg.shape, BF), jax.ShapeDtypeStruct(wu.shape, BF), jax.ShapeDtypeStruct(wd.shape, BF)]
    ospecs = [col, col, row]
    scratch = [pltpu.VMEM((tokens, d), BF), pltpu.VMEM((d, chunk), F32), pltpu.VMEM((d, chunk), F32), pltpu.VMEM((chunk, d), F32)]
    if carry:
        outs, ospecs = [jax.ShapeDtypeStruct(h.shape, BF)] + outs, [tok] + ospecs
        scratch += [pltpu.VMEM((tokens, d), F32)]
    return pl.pallas_call(
        functools.partial(backward_kernel, chunks=chunks, tile=tile, unroll=unroll, carry=carry),
        grid=(chunks,), in_specs=[tok, tok, col, col, row], out_specs=ospecs, out_shape=outs, scratch_shapes=scratch,
        compiler_params=pltpu.CompilerParams(dimension_semantics=("arbitrary",), vmem_limit_bytes=VM),
        cost_estimate=pl.CostEstimate(flops=(16 if carry else 12) * tokens * d * ff, bytes_accessed=4 * tokens * d * chunks, transcendentals=tokens * ff),
        name="backward_carry" if carry else "backward",
    )(h, dy, wg, wu, wd)


MESH = pl.DeviceIdType.MESH


class Place:
    def __init__(self, side, send_sems, recv_sems):
        self.side, self.send_sems, self.recv_sems, self.used = side, send_sems, recv_sems, 0
        me, rep = lax.axis_index("dp"), lax.axis_index("rep")
        self.at = (lax.div(me, side), lax.rem(me, side))
        self.parity = lax.rem(rep, 2)
        self.partner = rep + 1 - 2 * self.parity

    def along(self, axis, step):
        return lax.rem(self.at[axis] + step + self.side, self.side)

    def peer(self, axis, step):
        there = self.along(axis, step)
        return {"dp": there * self.side + self.at[1] if axis == 0 else self.at[0] * self.side + there}

    def greet(self, partner):
        barrier = pltpu.get_barrier_semaphore()
        peers = [self.peer(axis, step) for axis in (0, 1) for step in range(1, self.side)]
        peers += [{"rep": self.partner}] if partner else []
        for peer in peers:
            pl.semaphore_signal(barrier, inc=1, device_id=peer, device_id_type=MESH)
        pl.semaphore_wait(barrier, len(peers))

    def copy(self, src, dst, device):
        number, self.used = self.used, self.used + 1
        return pltpu.make_async_remote_copy(
            src_ref=src, dst_ref=dst, send_sem=self.send_sems.at[number], recv_sem=self.recv_sems.at[number], device_id=device, device_id_type=MESH
        )


def halves(parity, rows):
    return pl.ds(pl.multiple_of(parity * rows, rows), rows)


def gathering(place, blocks, wholes, local_sems):
    side, parity = place.side, place.parity
    parts = []
    for n, (block, whole) in enumerate(zip(blocks, wholes, strict=True)):
        half = block.shape[0] // 2
        if n < 2:
            parts.append((n, block, whole, halves(parity, half)))
        else:
            for axis in (0, 1):
                parts.append((axis, block, whole, pl.ds(pl.multiple_of(parity * half + axis * (half // 2), half // 2), half // 2)))

    def spot(whole, axis, i, j, rows):
        a, b = place.along(axis, -i), place.along(1 - axis, -j)
        return whole.at[a, b, rows] if axis == 0 else whole.at[b, a, rows]

    kept = []
    for n, (axis, block, whole, rows) in enumerate(parts):
        kept.append(pltpu.make_async_copy(block.at[rows], spot(whole, axis, 0, 0, rows), local_sems.at[n]))
        kept[-1].start()
    direct = [{} for _ in parts]
    for step in range(1, side):
        for n, (axis, block, whole, rows) in enumerate(parts):
            for way, which in ((axis, "near"), (1 - axis, "far")):
                copy = place.copy(block.at[rows], spot(whole, axis, 0, 0, rows), place.peer(way, step))
                copy.start()
                direct[n][which, step] = copy
    yield
    handed = [[] for _ in parts]
    for step in range(1, side):
        for n, (axis, block, whole, rows) in enumerate(parts):
            direct[n]["near", step].wait_recv()
            for other in range(1, side):
                here = spot(whole, axis, step, 0, rows)
                copy = place.copy(here, here, place.peer(1 - axis, other))
                copy.start()
                handed[n].append(copy)
    yield
    for n in range(len(parts)):
        kept[n].wait()
        for step in range(1, side):
            direct[n]["far", step].wait_recv()
        for copy in handed[n]:
            copy.wait_recv()
        if n == 2:
            continue
        block, whole = parts[n][1:3]
        mine = whole.at[:, :, halves(parity, block.shape[0] // 2)]
        across = place.copy(mine, mine, {"rep": place.partner})
        across.start()
        handed.append([across])
    yield
    for n in range(len(parts)):
        for copy in direct[n].values():
            copy.wait_send()
        for copy in handed[n]:
            copy.wait_send()
    for (across,) in handed[len(parts) :]:
        across.wait_send()
        across.wait_recv()


def gather_kernel(side, layers, *refs):
    blocks, wholes, (send_sems, recv_sems, local_sems) = refs[: 3 * layers], refs[3 * layers : 6 * layers], refs[6 * layers :]
    place = Place(side, send_sems, recv_sems)
    place.greet(True)
    runs = [gathering(place, blocks[3 * n : 3 * n + 3], wholes[3 * n : 3 * n + 3], local_sems.at[n]) for n in range(layers)]
    for _ in range(4):
        for run in runs:
            next(run, None)


def gather(side, blocks, number):
    layers = len(blocks) // 3
    copies = layers * (4 * (side * side - 1) + 3)
    return pl.pallas_call(
        functools.partial(gather_kernel, side, layers),
        in_specs=[pl.BlockSpec(memory_space=pltpu.VMEM)] * len(blocks),
        out_specs=[pl.BlockSpec(memory_space=pltpu.HBM)] * len(blocks),
        out_shape=[jax.ShapeDtypeStruct((side, side, *b.shape), b.dtype) for b in blocks],
        scratch_shapes=[pltpu.SemaphoreType.DMA((copies,)), pltpu.SemaphoreType.DMA((copies,)), pltpu.SemaphoreType.DMA((layers, 4))],
        compiler_params=pltpu.CompilerParams(collective_id=number, has_side_effects=True),
        name=f"gather_{number}",
    )(*blocks)


def scatter_parts(shapes):
    parts = []
    for n, (rows, columns) in enumerate(shapes):
        parts += [(n, n, 0, rows, columns)] if n < 2 else [(axis, n, axis * (rows // 2), rows // 2, columns) for axis in (0, 1)]
    return parts


def scatter_scratch(side, shapes):
    scratch = []
    for _, _, _, rows, columns in scatter_parts(shapes):
        scratch += [pltpu.VMEM((side, side, rows, columns), BF), pltpu.VMEM((side, rows, columns), BF), pltpu.VMEM((side - 1, rows, columns), BF)]
    return scratch + [pltpu.SemaphoreType.DMA((len(scratch) // 3,))]


def scattering(place, terms, outs, scratch):
    side = place.side
    local_sems = scratch[-1]
    parts = scatter_parts([out.shape for out in outs])

    def wide(ref, *index):
        return ref[index].astype(F32)

    work = []
    for n, (axis, matrix, start, rows, columns) in enumerate(parts):
        within = pl.ds(start, rows)
        first, partial, second = scratch[3 * n : 3 * n + 3]

        def line(step, axis=axis, term=terms[matrix], within=within):
            there = place.along(axis, step)
            return term.at[there, :, within] if axis == 0 else term.at[:, there, within]

        own = pltpu.make_async_copy(line(0), first.at[0], local_sems.at[n])
        own.start()
        copies = []
        for step in range(1, side):
            copies.append(place.copy(line(step), first.at[step], place.peer(axis, step)))
            copies[-1].start()
        work.append((axis, outs[matrix], within, first, partial, second, own, copies))
    yield
    later = []
    for axis, out, within, first, partial, second, own, copies in work:
        own.wait()
        for copy in copies:
            copy.wait_recv()

        def add(k, _, first=first, partial=partial):
            partial[k] = sum(wide(first, step, k) for step in range(side)).astype(BF)
            return 0

        lax.fori_loop(0, side, add, 0)
        later.append([])
        for step in range(1, side):
            copy = place.copy(partial.at[place.along(1 - axis, step)], second.at[step - 1], place.peer(1 - axis, step))
            copy.start()
            later[-1].append(copy)
    yield
    for (axis, out, within, first, partial, second, own, copies), more in zip(work, later, strict=True):
        for copy in more:
            copy.wait_recv()
        total = wide(partial, place.at[1 - axis])
        for step in range(side - 1):
            total += wide(second, step)
        out[within, :] = total.astype(BF)
        for copy in copies + more:
            copy.wait_send()


def scatter_kernel(side, layers, *refs):
    terms, outs, scratch = refs[: 3 * layers], refs[3 * layers : 6 * layers], refs[6 * layers :]
    place = Place(side, *scratch[:2])
    place.greet(False)
    each = (len(scratch) - 2) // layers
    runs = [scattering(place, terms[3 * n : 3 * n + 3], outs[3 * n : 3 * n + 3], scratch[2 + each * n : 2 + each * (n + 1)]) for n in range(layers)]
    for _ in range(3):
        for run in runs:
            next(run, None)


def scatter(side, terms, number):
    layers = len(terms) // 3
    shapes = [(t.shape[0] // side**2, t.shape[1]) for t in terms]
    copies = layers * 4 * 2 * (side - 1)
    scratch = [pltpu.SemaphoreType.DMA((copies,)), pltpu.SemaphoreType.DMA((copies,))]
    for n in range(layers):
        scratch += scatter_scratch(side, shapes[3 * n : 3 * n + 3])
    return pl.pallas_call(
        functools.partial(scatter_kernel, side, layers),
        in_specs=[pl.BlockSpec(memory_space=pltpu.HBM)] * len(terms),
        out_specs=[pl.BlockSpec(memory_space=pltpu.VMEM)] * len(terms),
        out_shape=[jax.ShapeDtypeStruct(s, BF) for s in shapes],
        scratch_shapes=scratch,
        compiler_params=pltpu.CompilerParams(collective_id=number, has_side_effects=True, vmem_limit_bytes=48 * 2**20),
        name=f"scatter_{number}",
    )(*(t.reshape(side, side, *s) for t, s in zip(terms, shapes, strict=True)))


NAMES = ("w_gate", "w_up", "w_down")


def adamw(w, m, v, g):
    m = 0.9 * m + 0.1 * g
    v = 0.95 * v + 0.05 * g * g
    step = m * lax.rsqrt(v + 1e-8) + 0.1 * w
    return (w - 0.02 * step).astype(BF), m, v


def solution(mesh):
    side = math.isqrt(mesh.shape["dp"])

    def step(x, dy, *arrays):
        weights, m, v = (arrays[i : i + 3] for i in (0, 3, 6))
        layers = weights[0].shape[0]
        h, dh = x[0], dy[0]
        wholes = gather(side, [w[number] for number in range(layers) for w in weights], 1)
        wholes = [w.reshape(-1, w.shape[-1]) for w in wholes]
        wholes = [wholes[3 * number : 3 * number + 3] for number in range(layers)]
        kept = [h]
        for number in range(layers - 1):
            kept.append(forward(kept[-1], *wholes[number]))
        terms = [None] * layers
        for number in reversed(range(layers)):
            if number:
                dh, *terms[number] = backward(kept[number], dh, *wholes[number], True)
            else:
                terms[number] = backward(kept[number], dh, *wholes[number], False)
        mine = scatter(side, sum((list(t) for t in terms), []), 2)
        gradients = [jnp.stack(mine[i::3]).astype(F32) for i in range(3)]
        new = [adamw(w.astype(F32), m, v, g) for w, m, v, g in zip(weights, m, v, gradients, strict=True)]
        return tuple(one[which] for which in range(3) for one in new)

    states, cut = P(("rep", "dp"), None, None), P(None, "dp", None)
    return jax.shard_map(
        step,
        mesh=mesh,
        in_specs=(states, states) + (cut,) * 9,
        out_specs=(P("rep", "dp", None),) * 9,
        check_vma=False,
    )
```

time: 808 us -> 375 us (0.46)
  waiting for transfers between devices: 427 us -> 0 us
  Pallas kernels: 0 us -> 363 us
  matrix products: 324 us -> 0 us
  between operations: 14.7 us -> 0.73 us
  local copies, waits for them, and re-layouts: 20 us -> 7.29 us
  other arithmetic: 12.6 us -> 3.56 us
    pallas_call x0 -> x5, Pallas kernels: none -> 363 us  [the longest x2 174 us: backward(): pl.pallas_call(functools.partial(backward_kernel, chunks=chunks, tile=til...]
    dot_general x15 -> x0, matrix products: 324 us -> none  [the longest x5 125 us: layer(): gate = jnp.dot(a, w['w_gate'], preferred_element_type=jnp.float32)]
    reduce_scatter x6 -> x0, waiting for transfers between devices: 294 us -> none  [step(): lax.psum_scatter(by_w[name], 'dp', scatter_dimension=0, tiled=True)]
    all_gather x6 -> x0, waiting for transfers between devices: 131 us -> none  [fetched(): lax.all_gather(w[number], 'dp', axis=0, tiled=True)]
    unnamed x42 -> x22, local copies, waits for them, and re-layouts: 14.9 us -> 3.71 us
  transfers between devices with their start and end apart: 12 -> 0, of which waited for: 11 -> 0; matrix products, arithmetic and copies ran while one was open for 32% -> 0% of each run, Pallas kernels for 0% -> 0%
where the time goes in v1:
time: 375 us; the launch traced here: 374 us
  Pallas kernels  363 us (97%)
  local copies, waits for them, and re-layouts  7.29 us (2%)
    pallas_call x2, Pallas kernels, backward(): pl.pallas_call(functools.partial(backward_kernel, chunks=chunks, tile=til...  174 us
    pallas_call x1, Pallas kernels, scatter(): pl.pallas_call(functools.partial(scatter_kernel, side, layers), in_specs=...  89.3 us
    pallas_call x1, Pallas kernels, gather(): pl.pallas_call(functools.partial(gather_kernel, side, layers), in_specs=[...  59.9 us
    pallas_call x1, Pallas kernels, forward(): pl.pallas_call(functools.partial(forward_kernel, chunks=chunks, tile=tile...  39.8 us

profile of v1, /device:TPU:97, one launch (start us, length us, event | category | flops | bytes accessed | tf_op | source)
XLA Modules:
  0.0 374.3 jit_solution(12030704583149254396)
XLA Ops:
  0.6 1.7 slice_bitcast_fusion
  2.3 1.9 slice_bitcast_fusion.1
  4.2 59.9 %gather_1.1 = (bf16[4,4,32,2048]{3,2,1,0:T(8,128)(2,1)}, bf16[4,4,32,2048]{3,2,1,0:T(8,128)(2,1)}, bf16[4,4,128,512]{3,2,1,0:T(8,128)(2,1)}, bf16[4,4,32,2048]{3...) custom-call(bf16[32,2048]{1,0:T(8,128)(2,1)} %get-tuple-element.62.refs_0_, ...), custom_call_target="tpu_custom_call" | custom-call | tf_op jit(solution)/shard_map/gather_1/pallas_call | solution.py:235
  64.1 39.8 %forward.1.h_ref = bf16[4096,512]{1,0:T(8,128)(2,1)} custom-call(bf16[4096,512]{1,0:T(8,128)(2,1)} %bitcast.45, bf16[512,2048]{1,0:T(8,128)(2,1)} %bitcast.47, bf16[512,2048]{1,0:T(8,128)(2,1)} %bitcast.49, bf16[2048,512]{1,0:T(8,128)(2,1)} %bitcast.51), custom_call_target="tpu_custom_call" | custom-call | flops 25769803776 | bytes 33554432 | tf_op jit(solution)/shard_map/forward/pallas_call | solution.py:54
  104.0 98.1 %backward_carry.1 = (bf16[4096,512]{1,0:T(8,128)(2,1)}, bf16[512,2048]{1,0:T(8,128)(2,1)}, bf16[512,2048]{1,0:T(8,128)(2,1)}, bf16[2048,512]{1,0:T(8,128)(2,1)}) custom-call(bf16[4096,512]{1,0:T(8,128)(2,1)} %forward.1.h_ref, bf16[4096,512]{1,0:T(8,128)(2,1)} %bitcast.44, bf16[512,2048]{1,0:T(8,128)(2,1)} %bitcast.53, bf16[512,2048]{1,0:T(8,128)(2,1)} %bitcast.54, ...), custom_call_target="tpu_custom_call" | custom-call | flops 68719476736 | bytes 33554432 | tf_op jit(solution)/shard_map/backward_carry/pallas_call | solution.py:115
  202.1 75.5 %backward.1 = (bf16[512,2048]{1,0:T(8,128)(2,1)}, bf16[512,2048]{1,0:T(8,128)(2,1)}, bf16[2048,512]{1,0:T(8,128)(2,1)}) custom-call(bf16[4096,512]{1,0:T(8,128)(2,1)} %bitcast.46, bf16[4096,512]{1,0:T(8,128)(2,1)} %get-tuple-element.34.dy_ref, bf16[512,2048]{1,0:T(8,128)(2,1)} %bitcast.48, bf16[512,2048]{1,0:T(8,128)(2,1)} %bitcast.50, ...), custom_call_target="tpu_custom_call" | custom-call | flops 51539607552 | bytes 33554432 | tf_op jit(solution)/shard_map/backward/pallas_call | solution.py:115
  277.6 0.0 copy-start
  277.7 1.6 copy-done
  279.2 0.0 copy-start.1
  279.2 1.6 copy-done.1
  280.8 0.0 copy-start.3
  280.8 0.0 copy-start.5
  280.8 0.0 copy-start.6
  280.8 89.3 %scatter_2.1 = (bf16[32,2048]{1,0:T(8,128)(2,1)S(1)}, bf16[32,2048]{1,0:T(8,128)(2,1)S(1)}, bf16[128,512]{1,0:T(8,128)(2,1)S(1)}, bf16[32,2048]{1,0:T(8,128)(2,1...) custom-call(bf16[4,4,32,2048]{3,2,1,0:T(8,128)(2,1)S(1)} %bitcast.32, ...), custom_call_target="tpu_custom_call" | custom-call | tf_op jit(solution)/shard_map/scatter_2/pallas_call | solution.py:331
  370.2 0.0 copy-start.4
  370.2 0.0 copy-start.7
  370.2 0.0 copy-start.8
  370.2 0.0 copy-done.3
  370.2 0.0 copy-done.5
  370.2 0.0 copy-done.6
  370.2 1.2 fusion.2
  371.4 0.0 copy-start.2
  371.4 0.0 copy-start.9
  371.4 0.0 copy-start.10
  371.4 0.0 copy-done.4
  371.4 0.0 copy-done.7
  371.4 0.5 copy-done.8
  371.9 1.2 fusion.6
  373.1 0.0 copy-done.2
  373.1 0.0 copy-done.9
  373.1 0.0 copy-done.10
  373.1 1.2 fusion.10
Async XLA Ops:
  277.6 1.6 copy-start
  279.2 1.6 copy-start.1
  280.8 89.4 %copy-start.3 = (bf16[2,32,2048]{2,1,0:T(8,128)(2,1)S(1)}, bf16[2,32,2048]{2,1,0:T(8,128)(2,1)}, u32[]{:S(2)}) copy-start(bf16[2,32,2048]{2,1,0:T(8,128)(2,1)} %param.13) | copy-start | bytes 786436
  280.8 89.4 %copy-start.5 = (f32[2,32,2048]{2,1,0:T(8,128)S(1)}, f32[2,32,2048]{2,1,0:T(8,128)}, u32[]{:S(2)}) copy-start(f32[2,32,2048]{2,1,0:T(8,128)} %param.19) | copy-start | bytes 1572868
  280.8 89.4 %copy-start.6 = (f32[2,32,2048]{2,1,0:T(8,128)S(1)}, f32[2,32,2048]{2,1,0:T(8,128)}, u32[]{:S(2)}) copy-start(f32[2,32,2048]{2,1,0:T(8,128)} %param.16) | copy-start | bytes 1572868
  370.2 1.3 copy-start.4
  370.2 1.2 copy-start.7
  370.2 1.7 copy-start.8
  371.4 1.7 copy-start.2
  371.4 1.7 copy-start.9
  371.4 1.7 copy-start.10

commit v2 on v0

v2 whole, which is shorter than its diff:
```python
import functools
import math

import jax
import jax.numpy as jnp
from jax import lax
from jax.experimental import pallas as pl
from jax.experimental.pallas import tpu as pltpu
from jax.sharding import PartitionSpec as P

BF, F32 = jnp.bfloat16, jnp.float32
VMEM_LIMIT = 63 * 2**20
MESH = pl.DeviceIdType.MESH
HBM = pl.BlockSpec(memory_space=pltpu.HBM)
VMEM = pl.BlockSpec(memory_space=pltpu.VMEM)
DMA = pltpu.SemaphoreType.DMA


class Place:
    def __init__(self, side, send_sems, recv_sems):
        self.side, self.send_sems, self.recv_sems = side, send_sems, recv_sems
        me, rep = lax.axis_index("dp"), lax.axis_index("rep")
        self.at = (lax.div(me, side), lax.rem(me, side))
        self.parity = lax.rem(rep, 2)
        self.partner = {"rep": rep + 1 - 2 * self.parity}

    def along(self, axis, step):
        return lax.rem(self.at[axis] + step + self.side, self.side)

    def peer(self, axis, step):
        there = self.along(axis, step)
        return {"dp": there * self.side + self.at[1] if axis == 0 else self.at[0] * self.side + there}

    def greet(self, partner):
        barrier = pltpu.get_barrier_semaphore()
        peers = [self.peer(axis, step) for axis in (0, 1) for step in range(1, self.side)]
        peers += [self.partner] if partner else []
        for peer in peers:
            pl.semaphore_signal(barrier, inc=1, device_id=peer, device_id_type=MESH)
        pl.semaphore_wait(barrier, len(peers))

    def copy(self, number, src, dst, device):
        return pltpu.make_async_remote_copy(
            src_ref=src, dst_ref=dst, send_sem=self.send_sems.at[number], recv_sem=self.recv_sems.at[number], device_id=device, device_id_type=MESH
        )


def span(start, size):
    return pl.ds(pl.multiple_of(start * size, size), size)


class Gathering:
    @staticmethod
    def copies(side):
        return 4 * (side * side - 1) + 3

    def __init__(self, place, blocks, wholes, local_sems):
        self.place, self.blocks, self.wholes, self.local_sems = place, blocks, wholes, local_sems

    def made(self):
        place, side, parity = self.place, self.place.side, self.place.parity
        parts = []
        for n, block in enumerate(self.blocks):
            half = block.shape[0] // 2
            if n < 2:
                parts.append((n, n, span(parity, half)))
            else:
                parts += [(axis, n, span(2 * parity + axis, half // 2)) for axis in (0, 1)]

        def spot(matrix, axis, behind, rows):
            a, b = place.along(axis, -behind), place.at[1 - axis]
            return self.wholes[matrix].at[a, b, rows] if axis == 0 else self.wholes[matrix].at[b, a, rows]

        kept, near, far, handed, number = [], {}, {}, {}, 0
        for n, (axis, matrix, rows) in enumerate(parts):
            src, own = self.blocks[matrix].at[rows], spot(matrix, axis, 0, rows)
            kept.append(pltpu.make_async_copy(src, own, self.local_sems.at[n]))
            for step in range(1, side):
                near[n, step] = place.copy(number, src, own, place.peer(axis, step))
                far[n, step] = place.copy(number + 1, src, own, place.peer(1 - axis, step))
                number += 2
                here = spot(matrix, axis, step, rows)
                for other in range(1, side):
                    handed[n, step, other] = place.copy(number, here, here, place.peer(1 - axis, other))
                    number += 1
        across = []
        for block, whole in zip(self.blocks, self.wholes, strict=True):
            mine = whole.at[:, :, span(parity, block.shape[0] // 2)]
            across.append(place.copy(number, mine, mine, place.partner))
            number += 1
        return kept, near, far, handed, across

    def send(self):
        kept, near, far, _, _ = self.made()
        for copy in kept:
            copy.start()
        for step in range(1, self.place.side):
            for n in range(len(kept)):
                near[n, step].start()
                far[n, step].start()

    def hand_on(self):
        kept, near, _, handed, _ = self.made()
        for step in range(1, self.place.side):
            for n in range(len(kept)):
                near[n, step].wait_recv()
                for other in range(1, self.place.side):
                    handed[n, step, other].start()

    def swap(self):
        kept, _, far, handed, across = self.made()
        for n, copy in enumerate(kept):
            copy.wait()
            for (part, *_), other in [*far.items(), *handed.items()]:
                if part == n:
                    other.wait_recv()
            if n != 2:
                across[min(n, 2)].start()

    def finish(self):
        _, near, far, handed, across = self.made()
        for copy in [*near.values(), *far.values(), *handed.values()]:
            copy.wait_send()
        for copy in across:
            copy.wait_send()
            copy.wait_recv()


def gather_kernel(side, layer, g, u, d, g_whole, u_whole, d_whole, send_sems, recv_sems, local_sems):
    place = Place(side, send_sems, recv_sems)
    run = Gathering(place, [block.at[layer] for block in (g, u, d)], (g_whole, u_whole, d_whole), local_sems)
    place.greet(True)
    run.send()
    run.hand_on()
    run.swap()
    run.finish()


def wholes_of(side, weights):
    return [jax.ShapeDtypeStruct((side, side, *w.shape[1:]), w.dtype) for w in weights]


def gather_sems(side):
    copies = Gathering.copies(side)
    return [DMA((copies,)), DMA((copies,)), DMA((4,))]


def gather(side, layer, weights, number):
    return pl.pallas_call(
        functools.partial(gather_kernel, side, layer),
        in_specs=[VMEM] * 3,
        out_specs=[HBM] * 3,
        out_shape=wholes_of(side, weights),
        scratch_shapes=gather_sems(side),
        compiler_params=pltpu.CompilerParams(collective_id=number, has_side_effects=True),
        name=f"gather_{number}",
    )(*weights)


class Scattering:
    @staticmethod
    def parts(shapes):
        parts = []
        for n, (rows, columns) in enumerate(shapes):
            parts += [(n, n, 0, rows, columns)] if n < 2 else [(axis, n, axis * (rows // 2), rows // 2, columns) for axis in (0, 1)]
        return parts

    @staticmethod
    def copies(side, pieces):
        return (side - 1) * (2 * pieces + 2 + 4)

    @classmethod
    def scratch(cls, side, shapes):
        scratch = []
        for _, _, _, rows, columns in cls.parts(shapes):
            scratch += [pltpu.VMEM((side, side, rows, columns), BF), pltpu.VMEM((side, rows, columns), BF), pltpu.VMEM((side - 1, rows, columns), BF)]
        return scratch + [DMA((4,))]

    def __init__(self, place, terms, outs, scratch, pieces, base, local):
        self.place, self.terms, self.outs, self.pieces, self.base, self.local = place, terms, outs, pieces, base, local
        self.split = self.parts([out.shape for out in outs])
        self.first, self.partial, self.second, self.local_sems = scratch[0:12:3], scratch[1:12:3], scratch[2:12:3], scratch[12]

    def line(self, part, step, columns):
        axis, matrix, start, rows, _ = self.split[part]
        there, within = self.place.along(axis, step), pl.ds(start, rows)
        return self.terms[matrix].at[there, :, within, columns] if axis == 0 else self.terms[matrix].at[:, there, within, columns]

    def near(self, part, piece=0):
        steps, width = self.place.side - 1, self.split[part][4]
        if part < 2:
            columns, number = span(piece, width // self.pieces), self.base + steps * (part * self.pieces + piece)
        else:
            columns, number = pl.ds(0, width), self.base + steps * (2 * self.pieces + part - 2)
        axis = self.split[part][0]
        return [
            self.place.copy(number + step - 1, self.line(part, step, columns), self.first[part].at[step, :, :, columns], self.place.peer(axis, step))
            for step in range(1, steps + 1)
        ]

    def own(self, part):
        return pltpu.make_async_copy(self.line(part, 0, pl.ds(0, self.split[part][4])), self.first[part].at[0], self.local_sems.at[part])

    def far(self, part):
        steps, axis = self.place.side - 1, self.split[part][0]
        number = self.base + steps * (2 * self.pieces + 2 + part)
        return [
            self.place.copy(
                number + step - 1, self.partial[part].at[self.place.along(1 - axis, step)], self.second[part].at[step - 1], self.place.peer(1 - axis, step)
            )
            for step in range(1, steps + 1)
        ]

    def pieces_of(self, part):
        return range(self.pieces if part < 2 else 1)

    def send(self, part, piece=0):
        if not self.local:
            self.own(part).start()
        for copy in self.near(part, piece):
            copy.start()

    def add(self, part):
        axis, matrix, start, rows, _ = self.split[part]
        first, partial, side = self.first[part], self.partial[part], self.place.side
        if not self.local:
            self.own(part).wait()
        for piece in self.pieces_of(part):
            for copy in self.near(part, piece):
                copy.wait_recv()
        here, within = self.place.at[axis], pl.ds(start, rows)

        def one(k, _):
            if not self.local:
                total = first[0, k].astype(F32)
            else:
                total = (self.terms[matrix][here, k, within] if axis == 0 else self.terms[matrix][k, here, within]).astype(F32)
            for step in range(1, side):
                total += first[step, k].astype(F32)
            partial[k] = total.astype(BF)
            return 0

        lax.fori_loop(0, side, one, 0)
        for copy in self.far(part):
            copy.start()

    def finish(self, part):
        axis, matrix, start, rows, _ = self.split[part]
        for copy in self.far(part):
            copy.wait_recv()
        total = self.partial[part][self.place.at[1 - axis]].astype(F32)
        for step in range(self.place.side - 1):
            total += self.second[part][step].astype(F32)
        self.outs[matrix][pl.ds(start, rows), :] = total.astype(BF)
        for piece in self.pieces_of(part):
            for copy in self.near(part, piece):
                copy.wait_send()
        for copy in self.far(part):
            copy.wait_send()


def dot(a, b, ca=1, cb=0):
    return lax.dot_general(a, b, (((ca,), (cb,)), ((), ())), preferred_element_type=F32)


def scale_of(wide):
    return lax.rsqrt(jnp.mean(wide * wide, -1, keepdims=True) + 1e-6)


def over(tokens, tile, unroll, body):
    def step(t, _):
        body(span(t, tile))
        return 0

    lax.fori_loop(0, tokens // tile, step, 0, unroll=unroll)


def prepare(h_ref, a_ref, total):
    def first(rows):
        wide = h_ref[rows, :].astype(F32)
        a_ref[rows, :] = (wide * scale_of(wide)).astype(BF)
        if total is not None:
            total[rows, :] = jnp.zeros((rows.size, total.shape[1]), F32)

    over(h_ref.shape[0], 256, 1, first)


def forward_kernel(
    side, chunks, layer, h_ref, wg_ref, wu_ref, wd_ref, g, u, d, out_ref, g_whole, u_whole, d_whole, a_ref, total, send_sems, recv_sems, local_sems
):
    c = pl.program_id(0)
    place = Place(side, send_sems, recv_sems)
    run = Gathering(place, [block.at[layer] for block in (g, u, d)], (g_whole, u_whole, d_whole), local_sems)

    @pl.when(c == 0)
    def _():
        place.greet(True)
        run.send()
        prepare(h_ref, a_ref, total)

    pl.when(c == 1)(run.hand_on)
    pl.when(c == chunks - 1)(run.swap)

    def main(rows):
        a = a_ref[rows, :]
        gate = dot(a, wg_ref[...])
        up = dot(a, wu_ref[...])
        act = (gate * jax.nn.sigmoid(gate) * up).astype(BF)
        total[rows, :] += dot(act, wd_ref[...])

    over(h_ref.shape[0], 512, 1, main)

    @pl.when(c == chunks - 1)
    def _():
        def last(rows):
            out_ref[rows, :] = h_ref[rows, :] + total[rows, :].astype(BF)

        over(h_ref.shape[0], 256, 1, last)
        run.finish()


def blocks_of(h, wg, chunks):
    tokens, width = h.shape
    chunk = wg.shape[1] // chunks
    tok = pl.BlockSpec((tokens, width), lambda c: (0, 0), pipeline_mode=pl.Buffered(1))
    return tok, pl.BlockSpec((width, chunk), lambda c: (0, c)), pl.BlockSpec((chunk, width), lambda c: (c, 0))


def forward(side, h, whole, weights, layer, number):
    (tokens, width), hidden, chunks = h.shape, whole[0].shape[1], side
    tok, col, row = blocks_of(h, whole[0], chunks)
    out, *wholes = pl.pallas_call(
        functools.partial(forward_kernel, side, chunks, layer),
        grid=(chunks,),
        in_specs=[tok, col, col, row] + [VMEM] * 3,
        out_specs=[tok] + [HBM] * 3,
        out_shape=[jax.ShapeDtypeStruct(h.shape, BF)] + wholes_of(side, weights),
        scratch_shapes=[pltpu.VMEM((tokens, width), BF), pltpu.VMEM((tokens, width), F32)] + gather_sems(side),
        compiler_params=pltpu.CompilerParams(
            dimension_semantics=("arbitrary",), vmem_limit_bytes=VMEM_LIMIT, collective_id=number, has_side_effects=True
        ),
        cost_estimate=pl.CostEstimate(flops=6 * tokens * width * hidden, bytes_accessed=4 * tokens * width, transcendentals=tokens * hidden),
        name="forward",
    )(h, *whole, *weights)
    return out, wholes


def chunk_terms(a_ref, dy_ref, wg_ref, wu_ref, wd_ref, sg, su, sd, total):
    for s in (sg, su, sd):
        s[...] = jnp.zeros_like(s)

    def main(rows):
        a, dy = a_ref[rows, :], dy_ref[rows, :]
        gate = dot(a, wg_ref[...])
        up = dot(a, wu_ref[...])
        dact = dot(dy, wd_ref[...], 1, 1).astype(BF).astype(F32)
        sig = jax.nn.sigmoid(gate)
        silu = gate * sig
        act = (silu * up).astype(BF)
        dup = (dact * silu).astype(BF)
        dgate = (dact * up * (sig + silu * (1 - sig))).astype(BF)
        sd[...] += dot(act, dy, 0, 0)
        sg[...] += dot(a, dgate, 0, 0)
        su[...] += dot(a, dup, 0, 0)
        if total is not None:
            total[rows, :] += dot(dgate, wg_ref[...], 1, 1) + dot(dup, wu_ref[...], 1, 1)

    over(a_ref.shape[0], 256, 2, main)


def carry_kernel(chunks, h_ref, dy_ref, wg_ref, wu_ref, wd_ref, dh_ref, gg_ref, gu_ref, gd_ref, a_ref, sg, su, sd, total):
    c = pl.program_id(0)
    pl.when(c == 0)(lambda: prepare(h_ref, a_ref, total))
    chunk_terms(a_ref, dy_ref, wg_ref, wu_ref, wd_ref, sg, su, sd, total)
    gd_ref[...] = sd[...].astype(BF)
    gg_ref[...] = sg[...].astype(BF)
    gu_ref[...] = su[...].astype(BF)

    @pl.when(c == chunks - 1)
    def _():
        def last(rows):
            wide = h_ref[rows, :].astype(F32)
            scale = scale_of(wide)
            da = total[rows, :].astype(BF).astype(F32)
            dwide = scale * (da - wide * (scale * scale * jnp.mean(da * wide, -1, keepdims=True)))
            dh_ref[rows, :] = dy_ref[rows, :] + dwide.astype(BF)

        over(h_ref.shape[0], 256, 1, last)


def sums_of(wg, wd, chunks):
    (width, hidden), chunk = wg.shape, wg.shape[1] // chunks
    return [pltpu.VMEM((width, chunk), F32), pltpu.VMEM((width, chunk), F32), pltpu.VMEM((chunk, width), F32)]


def backward_carry(side, h, dy, whole):
    (tokens, width), hidden, chunks = h.shape, whole[0].shape[1], side
    tok, col, row = blocks_of(h, whole[0], chunks)
    dh, *terms = pl.pallas_call(
        functools.partial(carry_kernel, chunks),
        grid=(chunks,),
        in_specs=[tok, tok, col, col, row],
        out_specs=[tok, col, col, row],
        out_shape=[jax.ShapeDtypeStruct(h.shape, BF)] + [jax.ShapeDtypeStruct(w.shape, BF) for w in whole],
        scratch_shapes=[pltpu.VMEM((tokens, width), BF), *sums_of(whole[0], whole[2], chunks), pltpu.VMEM((tokens, width), F32)],
        compiler_params=pltpu.CompilerParams(dimension_semantics=("arbitrary",), vmem_limit_bytes=VMEM_LIMIT),
        cost_estimate=pl.CostEstimate(flops=16 * tokens * width * hidden, bytes_accessed=6 * tokens * width, transcendentals=tokens * hidden),
        name="backward_carry",
    )(h, dy, *whole)
    return dh, terms


def last_kernel(side, chunks, h_ref, dy_ref, wg_ref, wu_ref, wd_ref, *rest):
    later, outs, outs_later, (a_ref, sg, su, sd), mine, (send_sems, recv_sems), scratch = (
        rest[0:3], rest[3:6], rest[6:9], rest[9:13], rest[13:16], rest[16:18], rest[18:]
    )
    half = len(scratch) // 2
    c = pl.program_id(0)
    place = Place(side, send_sems, recv_sems)
    above = Scattering(place, later, outs_later, scratch[:half], 1, 0, False)
    here = Scattering(place, mine, outs, scratch[half:], chunks, Scattering.copies(side, 1), True)
    parts = range(4)

    @pl.when(c == 0)
    def _():
        place.greet(False)
        for part in parts:
            above.send(part)
        prepare(h_ref, a_ref, None)

    @pl.when(c == chunks // 2)
    def _():
        for part in parts:
            above.add(part)

    @pl.when(c == chunks - 1)
    def _():
        for part in parts:
            above.finish(part)

    chunk_terms(a_ref, dy_ref, wg_ref, wu_ref, wd_ref, sg, su, sd, None)
    block = (side, side, mine[0].shape[2], sg.shape[1])
    mine[0][:, :, :, span(c, sg.shape[1])] = sg[...].astype(BF).reshape(block)
    mine[1][:, :, :, span(c, sg.shape[1])] = su[...].astype(BF).reshape(block)
    mine[2][c] = sd[...].astype(BF).reshape(mine[2].shape[1:])
    here.send(0, c)
    here.send(1, c)

    @pl.when(c == chunks - 1)
    def _():
        here.send(2)
        here.send(3)
        for part in parts:
            here.add(part)
        for part in parts:
            here.finish(part)


def backward_last(side, h, dy, whole, later, number):
    (tokens, width), hidden, chunks = h.shape, whole[0].shape[1], side
    tok, col, row = blocks_of(h, whole[0], chunks)
    shapes = [(t.shape[0] // side**2, t.shape[1]) for t in later]
    views = [(side, side, *s) for s in shapes]
    copies = Scattering.copies(side, 1) + Scattering.copies(side, chunks)
    found = pl.pallas_call(
        functools.partial(last_kernel, side, chunks),
        grid=(chunks,),
        in_specs=[tok, tok, col, col, row] + [HBM] * 3,
        out_specs=[VMEM] * 6,
        out_shape=[jax.ShapeDtypeStruct(s, BF) for s in shapes + shapes],
        scratch_shapes=[
            pltpu.VMEM((tokens, width), BF),
            *sums_of(whole[0], whole[2], chunks),
            *(pltpu.VMEM(v, BF) for v in views),
            DMA((copies,)),
            DMA((copies,)),
            *Scattering.scratch(side, shapes),
            *Scattering.scratch(side, shapes),
        ],
        compiler_params=pltpu.CompilerParams(
            dimension_semantics=("arbitrary",), vmem_limit_bytes=VMEM_LIMIT, collective_id=number, has_side_effects=True
        ),
        cost_estimate=pl.CostEstimate(flops=12 * tokens * width * hidden, bytes_accessed=4 * tokens * width, transcendentals=tokens * hidden),
        name="backward_last",
    )(h, dy, *whole, *(t.reshape(v) for t, v in zip(later, views, strict=True)))
    return found[:3], found[3:]


def adamw(w, m, v, g):
    m = 0.9 * m + 0.1 * g
    v = 0.95 * v + 0.05 * g * g
    step = m * lax.rsqrt(v + 1e-8) + 0.1 * w
    return (w - 0.02 * step).astype(BF), m, v


def solution(mesh):
    side = math.isqrt(mesh.shape["dp"])

    def step(x, dy, *arrays):
        weights, m, v = (arrays[i : i + 3] for i in (0, 3, 6))
        h = x[0]
        flat = lambda wholes: [w.reshape(-1, w.shape[-1]) for w in wholes]
        low = flat(gather(side, 0, weights, 1))
        above, high = forward(side, h, low, weights, 1, 2)
        dh, terms = backward_carry(side, above, dy[0], flat(high))
        mine = backward_last(side, h, dh, low, terms, 3)
        gradients = [jnp.stack([mine[number][i] for number in range(2)]).astype(F32) for i in range(3)]
        new = [adamw(w.astype(F32), m, v, g) for w, m, v, g in zip(weights, m, v, gradients, strict=True)]
        return tuple(one[which] for which in range(3) for one in new)

    states, cut = P(("rep", "dp"), None, None), P(None, "dp", None)
    return jax.shard_map(
        step,
        mesh=mesh,
        in_specs=(states, states) + (cut,) * 9,
        out_specs=(P("rep", "dp", None),) * 9,
        check_vma=False,
    )
```

time: 808 us -> 293 us (0.36); the launches traced: 799 us -> 293 us
  waiting for transfers between devices: 427 us -> 0 us
  matrix products: 324 us -> 0 us
  Pallas kernels: 0 us -> 287 us
  local copies, waits for them, and re-layouts: 20 us -> 0.05 us
  between operations: 14.7 us -> 0.8 us
    dot_general x15 -> x0, matrix products: 324 us -> none  [the longest x5 125 us: layer(): gate = jnp.dot(a, w['w_gate'], preferred_element_type=jnp.float32)]
    reduce_scatter x6 -> x0, waiting for transfers between devices: 294 us -> none  [step(): lax.psum_scatter(by_w[name], 'dp', scatter_dimension=0, tiled=True)]
    pallas_call x0 -> x4, Pallas kernels: none -> 287 us  [the longest x1 107 us: backward_last(): pl.pallas_call(functools.partial(last_kernel, side, chunks), grid=(chunks...]
    all_gather x6 -> x0, waiting for transfers between devices: 131 us -> none  [fetched(): lax.all_gather(w[number], 'dp', axis=0, tiled=True)]
    unnamed x42 -> x20, local copies, waits for them, and re-layouts: 14.9 us -> 0.05 us
  transfers between devices with their start and end apart: 12 -> 0, of which waited for: 11 -> 0; matrix products, arithmetic and copies ran while one was open for 32% -> 0% of each run, Pallas kernels for 0% -> 0%
where the time goes in v2:
time: 293 us
  Pallas kernels  287 us (98%)
  other arithmetic  5.3 us (2%)
    pallas_call x1, Pallas kernels, backward_last(): pl.pallas_call(functools.partial(last_kernel, side, chunks), grid=(chunks...  107 us
    pallas_call x1, Pallas kernels, backward_carry(): pl.pallas_call(functools.partial(carry_kernel, chunks), grid=(chunks,), i...  98.2 us
    pallas_call x1, Pallas kernels, forward(): pl.pallas_call(functools.partial(forward_kernel, side, chunks, layer), gr...  43.7 us
    pallas_call x1, Pallas kernels, gather(): pl.pallas_call(functools.partial(gather_kernel, side, layer), in_specs=[V...  37.6 us

profile of v2, /device:TPU:97, one launch (start us, length us, event | category | flops | bytes accessed | tf_op | source)
XLA Modules:
  0.0 292.8 jit_solution(10515703927365987271)
XLA Ops:
  0.6 37.6 %gather_1.1 = (bf16[4,4,32,2048]{3,2,1,0:T(8,128)(2,1)}, bf16[4,4,32,2048]{3,2,1,0:T(8,128)(2,1)}, bf16[4,4,128,512]{3,2,1,0:T(8,128)(2,1)}) custom-call(bf16[2,32,2048]{2,1,0:T(8,128)(2,1)} %g.3, bf16[2,32,2048]{2,1,0:T(8,128)(2,1)} %u.3, bf16[2,128,512]{2,1,0:T(8,128)(2,1)} %d.3), custom_call_target="tpu_custom_call" | custom-call | tf_op jit(solution)/shard_map/gather_1/pallas_call | solution.py:149
  38.3 43.7 %forward.1 = (bf16[4096,512]{1,0:T(8,128)(2,1)}, bf16[4,4,32,2048]{3,2,1,0:T(8,128)(2,1)}, bf16[4,4,32,2048]{3,2,1,0:T(8,128)(2,1)}, bf16[4,4,128,512]{3,2,1,0:T(8,128)(2,1)}) custom-call(bf16[4096,512]{1,0:T(8,128)(2,1)} %bitcast.24, bf16[512,2048]{1,0:T(8,128)(2,1)} %bitcast.26, bf16[512,2048]{1,0:T(8,128)(2,1)} %bitcast.28, bf16[2048,512]{1,0:T(8,128)(2,1)} %bitcast.30, ...), custom_call_target="tpu_custom_call" | custom-call | flops 25769803776 | bytes 8388608 | tf_op jit(solution)/shard_map/forward/pallas_call | solution.py:332
  82.0 98.2 %backward_carry.1 = (bf16[4096,512]{1,0:T(8,128)(2,1)}, bf16[512,2048]{1,0:T(8,128)(2,1)}, bf16[512,2048]{1,0:T(8,128)(2,1)}, bf16[2048,512]{1,0:T(8,128)(2,1)}) custom-call(bf16[4096,512]{1,0:T(8,128)(2,1)} %get-tuple-element.29.h_ref, bf16[4096,512]{1,0:T(8,128)(2,1)} %bitcast.23, bf16[512,2048]{1,0:T(8,128)(2,1)} %bitcast.35, bf16[512,2048]{1,0:T(8,128)(2,1)} %bitcast.36, ...), custom_call_target="tpu_custom_call" | custom-call | flops 68719476736 | bytes 12582912 | tf_op jit(solution)/shard_map/backward_carry/pallas_call | solution.py:399
  180.2 0.0 copy-start.2
  180.2 0.0 copy-start.3
  180.2 107.2 %backward_last.1 = (bf16[32,2048]{1,0:T(8,128)(2,1)}, bf16[32,2048]{1,0:T(8,128)(2,1)}, bf16[128,512]{1,0:T(8,128)(2,1)}, bf16[32,2048]{1,0:T(8,128)(2,1)}, bf16...) custom-call(bf16[4096,512]{1,0:T(8,128)(2,1)} %bitcast.25, bf16[4096,512]{1,0:T(8,128)(2,1)} %get-tuple-element.33.dy_ref, ...), custom_call_target="tpu_custom_call" | custom-call | flops 51539607552 | bytes 8388608 | tf_op jit(solution)/shard_map/backward_last/pallas_call | solution.py:465
  287.4 0.0 copy-start
  287.4 0.0 copy-start.1
  287.4 0.0 copy-start.4
  287.4 0.0 copy-start.5
  287.4 0.0 copy-start.6
  287.4 0.0 copy-start.7
  287.4 0.0 copy-start.8
  287.5 0.0 copy-start.9
  287.5 0.0 copy-done.2
  287.5 0.0 copy-done.3
  287.5 2.5 fusion.10
  290.0 0.0 copy-done
  290.0 0.0 copy-done.1
  290.0 0.0 copy-done.4
  290.0 0.0 copy-done.5
  290.0 0.0 copy-done.6
  290.0 0.0 copy-done.7
  290.0 0.0 copy-done.8
  290.1 0.0 copy-done.9
  290.1 2.8 fusion.2
Async XLA Ops:
  180.2 107.3 %copy-start.2 = (bf16[2,128,512]{2,1,0:T(8,128)(2,1)S(1)}, bf16[2,128,512]{2,1,0:T(8,128)(2,1)}, u32[]{:S(2)}) copy-start(bf16[2,128,512]{2,1,0:T(8,128)(2,1)} %d.3) | copy-start | bytes 786436
  180.2 107.3 %copy-start.3 = (f32[2,128,512]{2,1,0:T(8,128)S(1)}, f32[2,128,512]{2,1,0:T(8,128)}, u32[]{:S(2)}) copy-start(f32[2,128,512]{2,1,0:T(8,128)} %param.21) | copy-start | bytes 1572868
  287.4 2.6 copy-start
  287.4 2.6 copy-start.1
  287.4 2.6 copy-start.4
  287.4 2.6 copy-start.5
  287.4 2.6 copy-start.6
  287.4 2.6 copy-start.7
  287.4 2.6 copy-start.8
  287.5 2.6 copy-start.9

commit v3 on v2

--- a/solution.py
+++ b/solution.py
@@ -51,42 +51,44 @@
 
 class Gathering:
     @staticmethod
-    def copies(side):
-        return 4 * (side * side - 1) + 3
-
-    def __init__(self, place, blocks, wholes, local_sems):
-        self.place, self.blocks, self.wholes, self.local_sems = place, blocks, wholes, local_sems
+    def copies(side, parts, matrices):
+        return parts * (side * side - 1) + matrices
+
+    def __init__(self, place, items, local_sems, base=0):
+        self.place, self.items, self.local_sems, self.base = place, items, local_sems, base
 
     def made(self):
         place, side, parity = self.place, self.place.side, self.place.parity
         parts = []
-        for n, block in enumerate(self.blocks):
+        last = []
+        for block, whole, axis in self.items:
             half = block.shape[0] // 2
-            if n < 2:
-                parts.append((n, n, span(parity, half)))
+            if axis is None:
+                parts += [(one, block, whole, span(2 * parity + one, half // 2)) for one in (0, 1)]
             else:
-                parts += [(axis, n, span(2 * parity + axis, half // 2)) for axis in (0, 1)]
-
-        def spot(matrix, axis, behind, rows):
+                parts.append((axis, block, whole, span(parity, half)))
+            last.append(len(parts) - 1)
+
+        def spot(whole, axis, behind, rows):
             a, b = place.along(axis, -behind), place.at[1 - axis]
-            return self.wholes[matrix].at[a, b, rows] if axis == 0 else self.wholes[matrix].at[b, a, rows]
-
-        kept, near, far, handed, number = [], {}, {}, {}, 0
-        for n, (axis, matrix, rows) in enumerate(parts):
-            src, own = self.blocks[matrix].at[rows], spot(matrix, axis, 0, rows)
+            return whole.at[a, b, rows] if axis == 0 else whole.at[b, a, rows]
+
+        kept, near, far, handed, number = [], {}, {}, {}, self.base
+        for n, (axis, block, whole, rows) in enumerate(parts):
+            src, own = block.at[rows], spot(whole, axis, 0, rows)
             kept.append(pltpu.make_async_copy(src, own, self.local_sems.at[n]))
             for step in range(1, side):
                 near[n, step] = place.copy(number, src, own, place.peer(axis, step))
                 far[n, step] = place.copy(number + 1, src, own, place.peer(1 - axis, step))
                 number += 2
-                here = spot(matrix, axis, step, rows)
+                here = spot(whole, axis, step, rows)
                 for other in range(1, side):
                     handed[n, step, other] = place.copy(number, here, here, place.peer(1 - axis, other))
                     number += 1
-        across = []
-        for block, whole in zip(self.blocks, self.wholes, strict=True):
+        across = {}
+        for n, (block, whole, _) in zip(last, self.items, strict=True):
             mine = whole.at[:, :, span(parity, block.shape[0] // 2)]
-            across.append(place.copy(number, mine, mine, place.partner))
+            across[n] = place.copy(number, mine, mine, place.partner)
             number += 1
         return kept, near, far, handed, across
 
@@ -114,21 +116,21 @@
             for (part, *_), other in [*far.items(), *handed.items()]:
                 if part == n:
                     other.wait_recv()
-            if n != 2:
-                across[min(n, 2)].start()
+            if n in across:
+                across[n].start()
 
     def finish(self):
         _, near, far, handed, across = self.made()
         for copy in [*near.values(), *far.values(), *handed.values()]:
             copy.wait_send()
-        for copy in across:
+        for copy in across.values():
             copy.wait_send()
             copy.wait_recv()
 
 
-def gather_kernel(side, layer, g, u, d, g_whole, u_whole, d_whole, send_sems, recv_sems, local_sems):
+def gather_kernel(side, layer, g, u, g_whole, u_whole, send_sems, recv_sems, local_sems):
     place = Place(side, send_sems, recv_sems)
-    run = Gathering(place, [block.at[layer] for block in (g, u, d)], (g_whole, u_whole, d_whole), local_sems)
+    run = Gathering(place, [(g.at[layer], g_whole, 0), (u.at[layer], u_whole, 1)], local_sems)
     place.greet(True)
     run.send()
     run.hand_on()
@@ -140,18 +142,14 @@
     return [jax.ShapeDtypeStruct((side, side, *w.shape[1:]), w.dtype) for w in weights]
 
 
-def gather_sems(side):
-    copies = Gathering.copies(side)
-    return [DMA((copies,)), DMA((copies,)), DMA((4,))]
-
-
 def gather(side, layer, weights, number):
+    copies = Gathering.copies(side, 2, 2)
     return pl.pallas_call(
         functools.partial(gather_kernel, side, layer),
-        in_specs=[VMEM] * 3,
-        out_specs=[HBM] * 3,
+        in_specs=[VMEM] * 2,
+        out_specs=[HBM] * 2,
         out_shape=wholes_of(side, weights),
-        scratch_shapes=gather_sems(side),
+        scratch_shapes=[DMA((copies,)), DMA((copies,)), DMA((2,))],
         compiler_params=pltpu.CompilerParams(collective_id=number, has_side_effects=True),
         name=f"gather_{number}",
     )(*weights)
@@ -160,14 +158,13 @@
 class Scattering:
     @staticmethod
     def parts(shapes):
-        parts = []
-        for n, (rows, columns) in enumerate(shapes):
-            parts += [(n, n, 0, rows, columns)] if n < 2 else [(axis, n, axis * (rows // 2), rows // 2, columns) for axis in (0, 1)]
-        return parts
+        (rows, columns), (middle, _), (tall, narrow) = shapes
+        half = middle // 2
+        return [(0, 0, 0, rows, columns), (0, 1, 0, half, columns), (1, 1, half, half, columns), (1, 2, 0, tall, narrow)]
 
     @staticmethod
     def copies(side, pieces):
-        return (side - 1) * (2 * pieces + 2 + 4)
+        return (side - 1) * 8 * pieces
 
     @classmethod
     def scratch(cls, side, shapes):
@@ -181,38 +178,47 @@
         self.split = self.parts([out.shape for out in outs])
         self.first, self.partial, self.second, self.local_sems = scratch[0:12:3], scratch[1:12:3], scratch[2:12:3], scratch[12]
 
-    def line(self, part, step, columns):
+    def tall(self, part):
+        return self.split[part][1] == 2
+
+    def columns(self, part, piece):
+        width = self.split[part][4]
+        return pl.ds(0, width) if self.tall(part) else span(piece, width // self.pieces)
+
+    def line(self, part, step, columns, piece):
         axis, matrix, start, rows, _ = self.split[part]
         there, within = self.place.along(axis, step), pl.ds(start, rows)
-        return self.terms[matrix].at[there, :, within, columns] if axis == 0 else self.terms[matrix].at[:, there, within, columns]
-
-    def near(self, part, piece=0):
-        steps, width = self.place.side - 1, self.split[part][4]
-        if part < 2:
-            columns, number = span(piece, width // self.pieces), self.base + steps * (part * self.pieces + piece)
-        else:
-            columns, number = pl.ds(0, width), self.base + steps * (2 * self.pieces + part - 2)
-        axis = self.split[part][0]
-        return [
-            self.place.copy(number + step - 1, self.line(part, step, columns), self.first[part].at[step, :, :, columns], self.place.peer(axis, step))
-            for step in range(1, steps + 1)
-        ]
+        if axis == 0:
+            return self.terms[matrix].at[there, :, within, columns]
+        return self.terms[matrix].at[slice(None) if piece is None else piece, there, within, columns]
+
+    def near(self, part, piece):
+        steps, columns = self.place.side - 1, self.columns(part, piece)
+        number, which = self.base + steps * (part * self.pieces + piece), piece if self.tall(part) and self.pieces > 1 else None
+        axis, copies = self.split[part][0], []
+        for step in range(1, steps + 1):
+            first = self.first[part].at[step, :, :, columns] if which is None else self.first[part].at[step, which]
+            copies.append(self.place.copy(number + step - 1, self.line(part, step, columns, which), first, self.place.peer(axis, step)))
+        return copies
 
     def own(self, part):
-        return pltpu.make_async_copy(self.line(part, 0, pl.ds(0, self.split[part][4])), self.first[part].at[0], self.local_sems.at[part])
-
-    def far(self, part):
-        steps, axis = self.place.side - 1, self.split[part][0]
-        number = self.base + steps * (2 * self.pieces + 2 + part)
+        return pltpu.make_async_copy(self.line(part, 0, self.columns(part, 0), None), self.first[part].at[0], self.local_sems.at[part])
+
+    def far(self, part, piece):
+        steps, axis, columns = self.place.side - 1, self.split[part][0], self.columns(part, piece)
+        number = self.base + steps * (4 * self.pieces + part * self.pieces + piece)
         return [
             self.place.copy(
-                number + step - 1, self.partial[part].at[self.place.along(1 - axis, step)], self.second[part].at[step - 1], self.place.peer(1 - axis, step)
+                number + step - 1,
+                self.partial[part].at[self.place.along(1 - axis, step), :, columns],
+                self.second[part].at[step - 1, :, columns],
+                self.place.peer(1 - axis, step),
             )
             for step in range(1, steps + 1)
         ]
 
-    def pieces_of(self, part):
-        return range(self.pieces if part < 2 else 1)
+    def far_pieces(self, part):
+        return [self.pieces - 1] if self.tall(part) else range(self.pieces)
 
     def send(self, part, piece=0):
         if not self.local:
@@ -220,43 +226,48 @@
         for copy in self.near(part, piece):
             copy.start()
 
-    def add(self, part):
+    def add(self, part, piece=0):
         axis, matrix, start, rows, _ = self.split[part]
         first, partial, side = self.first[part], self.partial[part], self.place.side
+        here, within, columns = self.place.at[axis], pl.ds(start, rows), self.columns(part, piece)
         if not self.local:
             self.own(part).wait()
-        for piece in self.pieces_of(part):
-            for copy in self.near(part, piece):
-                copy.wait_recv()
-        here, within = self.place.at[axis], pl.ds(start, rows)
+        for copy in self.near(part, piece):
+            copy.wait_recv()
 
         def one(k, _):
             if not self.local:
-                total = first[0, k].astype(F32)
+                total = first[0, k, :, columns].astype(F32)
             else:
-                total = (self.terms[matrix][here, k, within] if axis == 0 else self.terms[matrix][k, here, within]).astype(F32)
+                total = (self.terms[matrix][here, k, within, columns] if axis == 0 else self.terms[matrix][k, here, within, columns]).astype(F32)
             for step in range(1, side):
-                total += first[step, k].astype(F32)
-            partial[k] = total.astype(BF)
+                total += first[step, k, :, columns].astype(F32)
+            partial[k, :, columns] = total.astype(BF)
             return 0
 
-        lax.fori_loop(0, side, one, 0)
-        for copy in self.far(part):
-            copy.start()
+        if self.tall(part) and self.pieces > 1:
+            one(piece, 0)
+        else:
+            lax.fori_loop(0, side, one, 0)
+        if piece in self.far_pieces(part):
+            for copy in self.far(part, piece):
+                copy.start()
 
     def finish(self, part):
         axis, matrix, start, rows, _ = self.split[part]
-        for copy in self.far(part):
-            copy.wait_recv()
+        for piece in self.far_pieces(part):
+            for copy in self.far(part, piece):
+                copy.wait_recv()
         total = self.partial[part][self.place.at[1 - axis]].astype(F32)
         for step in range(self.place.side - 1):
             total += self.second[part][step].astype(F32)
         self.outs[matrix][pl.ds(start, rows), :] = total.astype(BF)
-        for piece in self.pieces_of(part):
+        for piece in range(self.pieces):
             for copy in self.near(part, piece):
                 copy.wait_send()
-        for copy in self.far(part):
-            copy.wait_send()
+        for piece in self.far_pieces(part):
+            for copy in self.far(part, piece):
+                copy.wait_send()
 
 
 def dot(a, b, ca=1, cb=0):
@@ -285,38 +296,57 @@
     over(h_ref.shape[0], 256, 1, first)
 
 
-def forward_kernel(
-    side, chunks, layer, h_ref, wg_ref, wu_ref, wd_ref, g, u, d, out_ref, g_whole, u_whole, d_whole, a_ref, total, send_sems, recv_sems, local_sems
-):
+def forward_kernel(side, chunks, layer, h_ref, wg_ref, wu_ref, g, u, d, out_ref, *rest):
+    low_whole, g_whole, u_whole, d_whole, a_ref, act_ref, wd_ref, send_sems, recv_sems, local_sems, load_sem = rest
     c = pl.program_id(0)
     place = Place(side, send_sems, recv_sems)
-    run = Gathering(place, [block.at[layer] for block in (g, u, d)], (g_whole, u_whole, d_whole), local_sems)
+    low = Gathering(place, [(d.at[layer - 1], low_whole, None)], local_sems.at[0])
+    high = Gathering(
+        place,
+        [(g.at[layer], g_whole, 0), (u.at[layer], u_whole, 1), (d.at[layer], d_whole, None)],
+        local_sems.at[1],
+        Gathering.copies(side, 2, 1),
+    )
+    load = pltpu.make_async_copy(low_whole, wd_ref, load_sem)
 
     @pl.when(c == 0)
     def _():
         place.greet(True)
-        run.send()
-        prepare(h_ref, a_ref, total)
-
-    pl.when(c == 1)(run.hand_on)
-    pl.when(c == chunks - 1)(run.swap)
+        low.send()
+        high.send()
+        prepare(h_ref, a_ref, None)
+
+    @pl.when(c == 1)
+    def _():
+        low.hand_on()
+        high.hand_on()
+
+    pl.when(c == chunks - 2)(low.swap)
+
+    @pl.when(c == chunks - 1)
+    def _():
+        low.finish()
+        load.start()
+        high.swap()
 
     def main(rows):
         a = a_ref[rows, :]
         gate = dot(a, wg_ref[...])
         up = dot(a, wu_ref[...])
-        act = (gate * jax.nn.sigmoid(gate) * up).astype(BF)
-        total[rows, :] += dot(act, wd_ref[...])
+        act_ref[rows, span(c, wg_ref.shape[1])] = (gate * jax.nn.sigmoid(gate) * up).astype(BF)
 
     over(h_ref.shape[0], 512, 1, main)
 
     @pl.when(c == chunks - 1)
     def _():
+        load.wait()
+
         def last(rows):
-            out_ref[rows, :] = h_ref[rows, :] + total[rows, :].astype(BF)
-
-        over(h_ref.shape[0], 256, 1, last)
-        run.finish()
+            wd = wd_ref[...].reshape(act_ref.shape[1], h_ref.shape[1])
+            out_ref[rows, :] = h_ref[rows, :] + dot(act_ref[rows, :], wd).astype(BF)
+
+        over(h_ref.shape[0], 512, 1, last)
+        high.finish()
 
 
 def blocks_of(h, wg, chunks):
@@ -329,20 +359,30 @@
 def forward(side, h, whole, weights, layer, number):
     (tokens, width), hidden, chunks = h.shape, whole[0].shape[1], side
     tok, col, row = blocks_of(h, whole[0], chunks)
+    down, *_ = wholes_of(side, weights[2:])
+    copies = Gathering.copies(side, 2, 1) + Gathering.copies(side, 4, 3)
     out, *wholes = pl.pallas_call(
         functools.partial(forward_kernel, side, chunks, layer),
         grid=(chunks,),
-        in_specs=[tok, col, col, row] + [VMEM] * 3,
-        out_specs=[tok] + [HBM] * 3,
-        out_shape=[jax.ShapeDtypeStruct(h.shape, BF)] + wholes_of(side, weights),
-        scratch_shapes=[pltpu.VMEM((tokens, width), BF), pltpu.VMEM((tokens, width), F32)] + gather_sems(side),
+        in_specs=[tok, col, col] + [VMEM] * 3,
+        out_specs=[tok] + [HBM] * 4,
+        out_shape=[jax.ShapeDtypeStruct(h.shape, BF), down] + wholes_of(side, weights),
+        scratch_shapes=[
+            pltpu.VMEM((tokens, width), BF),
+            pltpu.VMEM((tokens, hidden), BF),
+            pltpu.VMEM(down.shape, BF),
+            DMA((copies,)),
+            DMA((copies,)),
+            DMA((2, 4)),
+            DMA(()),
+        ],
         compiler_params=pltpu.CompilerParams(
             dimension_semantics=("arbitrary",), vmem_limit_bytes=VMEM_LIMIT, collective_id=number, has_side_effects=True
         ),
         cost_estimate=pl.CostEstimate(flops=6 * tokens * width * hidden, bytes_accessed=4 * tokens * width, transcendentals=tokens * hidden),
         name="forward",
     )(h, *whole, *weights)
-    return out, wholes
+    return out, wholes[0], wholes[1:]
 
 
 def chunk_terms(a_ref, dy_ref, wg_ref, wu_ref, wd_ref, sg, su, sd, total):
@@ -437,21 +477,23 @@
     def _():
         for part in parts:
             above.finish(part)
+        for piece in range(chunks - 2):
+            for part in parts:
+                here.add(part, piece)
 
     chunk_terms(a_ref, dy_ref, wg_ref, wu_ref, wd_ref, sg, su, sd, None)
     block = (side, side, mine[0].shape[2], sg.shape[1])
     mine[0][:, :, :, span(c, sg.shape[1])] = sg[...].astype(BF).reshape(block)
     mine[1][:, :, :, span(c, sg.shape[1])] = su[...].astype(BF).reshape(block)
     mine[2][c] = sd[...].astype(BF).reshape(mine[2].shape[1:])
-    here.send(0, c)
-    here.send(1, c)
+    for part in parts:
+        here.send(part, c)
 
     @pl.when(c == chunks - 1)
     def _():
-        here.send(2)
-        here.send(3)
-        for part in parts:
-            here.add(part)
+        for piece in range(chunks - 2, chunks):
+            for part in parts:
+                here.add(part, piece)
         for part in parts:
             here.finish(part)
 
@@ -500,8 +542,9 @@
         weights, m, v = (arrays[i : i + 3] for i in (0, 3, 6))
         h = x[0]
         flat = lambda wholes: [w.reshape(-1, w.shape[-1]) for w in wholes]
-        low = flat(gather(side, 0, weights, 1))
-        above, high = forward(side, h, low, weights, 1, 2)
+        low = flat(gather(side, 0, weights[:2], 1))
+        above, down, high = forward(side, h, low, weights, 1, 2)
+        low += flat([down])
         dh, terms = backward_carry(side, above, dy[0], flat(high))
         mine = backward_last(side, h, dh, low, terms, 3)
         gradients = [jnp.stack([mine[number][i] for number in range(2)]).astype(F32) for i in range(3)]

time: 293 us -> 294 us (level)
    pallas_call x1, Pallas kernels: 43.7 us -> 54.3 us  [forward(): pl.pallas_call(functools.partial(forward_kernel, side, chunks, layer), gr...]
    pallas_call x1, Pallas kernels: 37.6 us -> 29.1 us  [gather(): pl.pallas_call(functools.partial(gather_kernel, side, layer), in_specs=[V...]
    pallas_call x1, Pallas kernels: 107 us -> 103 us  [backward_last(): pl.pallas_call(functools.partial(last_kernel, side, chunks), grid=(chunks...]
where the time goes in v3:
time: 294 us; the launch traced here: 291 us
  Pallas kernels  285 us (97%)
  other arithmetic  5.3 us (2%)
    pallas_call x1, Pallas kernels, backward_last(): pl.pallas_call(functools.partial(last_kernel, side, chunks), grid=(chunks...  103 us
    pallas_call x1, Pallas kernels, backward_carry(): pl.pallas_call(functools.partial(carry_kernel, chunks), grid=(chunks,), i...  98.2 us
    pallas_call x1, Pallas kernels, forward(): pl.pallas_call(functools.partial(forward_kernel, side, chunks, layer), gr...  54.3 us
    pallas_call x1, Pallas kernels, gather(): pl.pallas_call(functools.partial(gather_kernel, side, layer), in_specs=[V...  29.1 us

profile of v3, /device:TPU:97, one launch (start us, length us, event | category | flops | bytes accessed | tf_op | source)
XLA Modules:
  0.0 291.3 jit_solution(15802046896239281578)
XLA Ops:
  0.6 29.1 %gather_1.1 = (bf16[4,4,32,2048]{3,2,1,0:T(8,128)(2,1)}, bf16[4,4,32,2048]{3,2,1,0:T(8,128)(2,1)}) custom-call(bf16[2,32,2048]{2,1,0:T(8,128)(2,1)} %g.3, bf16[2,32,2048]{2,1,0:T(8,128)(2,1)} %u.3), custom_call_target="tpu_custom_call" | custom-call | tf_op jit(solution)/shard_map/gather_1/pallas_call | solution.py:147
  29.8 54.3 %forward.1 = (bf16[4096,512]{1,0:T(8,128)(2,1)}, bf16[4,4,128,512]{3,2,1,0:T(8,128)(2,1)}, bf16[4,4,32,2048]{3,2,1,0:T(8,128)(2,1)}, bf16[4,4,32,2048]{3,2,1,0:T(8,128)(2,1)}, bf16[4,4,128,512]{3,2,1,0:T(8,128)(2,1)}) custom-call(bf16[4096,512]{1,0:T(8,128)(2,1)} %bitcast.24, bf16[512,2048]{1,0:T(8,128)(2,1)} %bitcast.26, bf16[512,2048]{1,0:T(8,128)(2,1)} %bitcast.28, ...), custom_call_target="tpu_custom_call" | custom-call | flops 25769803776 | bytes 8388608 | tf_op jit(solution)/shard_map/forward/pallas_call | solution.py:364
  84.1 98.2 %backward_carry.1 = (bf16[4096,512]{1,0:T(8,128)(2,1)}, bf16[512,2048]{1,0:T(8,128)(2,1)}, bf16[512,2048]{1,0:T(8,128)(2,1)}, bf16[2048,512]{1,0:T(8,128)(2,1)}) custom-call(bf16[4096,512]{1,0:T(8,128)(2,1)} %get-tuple-element.28.h_ref, bf16[4096,512]{1,0:T(8,128)(2,1)} %bitcast.23, bf16[512,2048]{1,0:T(8,128)(2,1)} %bitcast.34, bf16[512,2048]{1,0:T(8,128)(2,1)} %bitcast.35, ...), custom_call_target="tpu_custom_call" | custom-call | flops 68719476736 | bytes 12582912 | tf_op jit(solution)/shard_map/backward_carry/pallas_call | solution.py:439
  182.3 0.0 copy-start.2
  182.3 0.0 copy-start.7
  182.3 103.5 %backward_last.1 = (bf16[32,2048]{1,0:T(8,128)(2,1)}, bf16[32,2048]{1,0:T(8,128)(2,1)}, bf16[128,512]{1,0:T(8,128)(2,1)}, bf16[32,2048]{1,0:T(8,128)(2,1)}, bf16...) custom-call(bf16[4096,512]{1,0:T(8,128)(2,1)} %bitcast.25, bf16[4096,512]{1,0:T(8,128)(2,1)} %get-tuple-element.32.dy_ref, ...), custom_call_target="tpu_custom_call" | custom-call | flops 51539607552 | bytes 8388608 | tf_op jit(solution)/shard_map/backward_last/pallas_call | solution.py:507
  285.8 0.0 copy-start
  285.8 0.0 copy-start.1
  285.8 0.0 copy-start.3
  285.8 0.0 copy-start.4
  285.9 0.0 copy-start.5
  285.9 0.0 copy-start.6
  285.9 0.0 copy-start.8
  285.9 0.0 copy-start.9
  285.9 0.0 copy-done.2
  285.9 0.0 copy-done.7
  285.9 2.5 fusion.10
  288.4 0.0 copy-done
  288.5 0.0 copy-done.1
  288.5 0.0 copy-done.3
  288.5 0.0 copy-done.4
  288.5 0.0 copy-done.5
  288.5 0.0 copy-done.6
  288.5 0.0 copy-done.8
  288.5 0.0 copy-done.9
  288.5 2.8 fusion.2
Async XLA Ops:
  182.3 103.6 %copy-start.2 = (f32[2,128,512]{2,1,0:T(8,128)S(1)}, f32[2,128,512]{2,1,0:T(8,128)}, u32[]{:S(2)}) copy-start(f32[2,128,512]{2,1,0:T(8,128)} %param.21) | copy-start | bytes 1572868
  182.3 103.6 %copy-start.7 = (bf16[2,128,512]{2,1,0:T(8,128)(2,1)S(1)}, bf16[2,128,512]{2,1,0:T(8,128)(2,1)}, u32[]{:S(2)}) copy-start(bf16[2,128,512]{2,1,0:T(8,128)(2,1)} %d.1) | copy-start | bytes 786436
  285.8 2.6 copy-start
  285.8 2.6 copy-start.1
  285.8 2.6 copy-start.3
  285.8 2.6 copy-start.4
  285.9 2.6 copy-start.5
  285.9 2.6 copy-start.6
  285.9 2.6 copy-start.8
  285.9 2.6 copy-start.9

commit v4 on v3

--- a/solution.py
+++ b/solution.py
@@ -173,9 +173,9 @@
             scratch += [pltpu.VMEM((side, side, rows, columns), BF), pltpu.VMEM((side, rows, columns), BF), pltpu.VMEM((side - 1, rows, columns), BF)]
         return scratch + [DMA((4,))]
 
-    def __init__(self, place, terms, outs, scratch, pieces, base, local):
+    def __init__(self, place, terms, outs, scratch, pieces, base, local, shapes):
         self.place, self.terms, self.outs, self.pieces, self.base, self.local = place, terms, outs, pieces, base, local
-        self.split = self.parts([out.shape for out in outs])
+        self.split = self.parts(shapes)
         self.first, self.partial, self.second, self.local_sems = scratch[0:12:3], scratch[1:12:3], scratch[2:12:3], scratch[12]
 
     def tall(self, part):
@@ -253,19 +253,22 @@
             for copy in self.far(part, piece):
                 copy.start()
 
-    def finish(self, part):
+    def finish(self, part, pieces=None):
         axis, matrix, start, rows, _ = self.split[part]
-        for piece in self.far_pieces(part):
+        pieces = range(self.pieces if pieces is None else pieces)
+        far = self.far_pieces(part) if self.tall(part) else pieces
+        for piece in far:
             for copy in self.far(part, piece):
                 copy.wait_recv()
-        total = self.partial[part][self.place.at[1 - axis]].astype(F32)
-        for step in range(self.place.side - 1):
-            total += self.second[part][step].astype(F32)
-        self.outs[matrix][pl.ds(start, rows), :] = total.astype(BF)
-        for piece in range(self.pieces):
+            columns = self.columns(part, piece)
+            total = self.partial[part][self.place.at[1 - axis], :, columns].astype(F32)
+            for step in range(self.place.side - 1):
+                total += self.second[part][step, :, columns].astype(F32)
+            self.outs[matrix][pl.ds(start, rows), columns] = total.astype(BF)
+        for piece in pieces:
             for copy in self.near(part, piece):
                 copy.wait_send()
-        for piece in self.far_pieces(part):
+        for piece in far:
             for copy in self.far(part, piece):
                 copy.wait_send()
 
@@ -327,7 +330,6 @@
     def _():
         low.finish()
         load.start()
-        high.swap()
 
     def main(rows):
         a = a_ref[rows, :]
@@ -340,6 +342,7 @@
     @pl.when(c == chunks - 1)
     def _():
         load.wait()
+        high.swap()
 
         def last(rows):
             wd = wd_ref[...].reshape(act_ref.shape[1], h_ref.shape[1])
@@ -408,16 +411,43 @@
     over(a_ref.shape[0], 256, 2, main)
 
 
-def carry_kernel(chunks, h_ref, dy_ref, wg_ref, wu_ref, wd_ref, dh_ref, gg_ref, gu_ref, gd_ref, a_ref, sg, su, sd, total):
+def carry_kernel(side, chunks, shapes, h_ref, dy_ref, wg_ref, wu_ref, wd_ref, dh_ref, gg_ref, gu_ref, gd_ref, eg_ref, eu_ref, *rest):
+    (a_ref, sg, su, sd, total), mine, (send_sems, recv_sems), scratch = rest[:5], rest[5:7], rest[7:9], rest[9:]
     c = pl.program_id(0)
-    pl.when(c == 0)(lambda: prepare(h_ref, a_ref, total))
+    place = Place(side, send_sems, recv_sems)
+    early = Scattering(place, (*mine, None), (eg_ref, eu_ref, None), scratch, chunks, 0, True, shapes)
+    parts = range(3)
+
+    @pl.when(c == 0)
+    def _():
+        place.greet(False)
+        prepare(h_ref, a_ref, total)
+
+    for piece in range(chunks - 2):
+
+        @pl.when(c == piece + 2)
+        def _(piece=piece):
+            for part in parts:
+                early.add(part, piece)
+
     chunk_terms(a_ref, dy_ref, wg_ref, wu_ref, wd_ref, sg, su, sd, total)
     gd_ref[...] = sd[...].astype(BF)
-    gg_ref[...] = sg[...].astype(BF)
-    gu_ref[...] = su[...].astype(BF)
+
+    @pl.when(c < chunks - 1)
+    def _():
+        block = (side, side, mine[0].shape[2], sg.shape[1])
+        mine[0][:, :, :, span(c, sg.shape[1])] = sg[...].astype(BF).reshape(block)
+        mine[1][:, :, :, span(c, sg.shape[1])] = su[...].astype(BF).reshape(block)
+        for part in parts:
+            early.send(part, c)
 
     @pl.when(c == chunks - 1)
     def _():
+        for part in parts:
+            early.add(part, chunks - 2)
+        gg_ref[...] = sg[...].astype(BF)
+        gu_ref[...] = su[...].astype(BF)
+
         def last(rows):
             wide = h_ref[rows, :].astype(F32)
             scale = scale_of(wide)
@@ -426,6 +456,8 @@
             dh_ref[rows, :] = dy_ref[rows, :] + dwide.astype(BF)
 
         over(h_ref.shape[0], 256, 1, last)
+        for part in parts:
+            early.finish(part, chunks - 1)
 
 
 def sums_of(wg, wd, chunks):
@@ -433,32 +465,52 @@
     return [pltpu.VMEM((width, chunk), F32), pltpu.VMEM((width, chunk), F32), pltpu.VMEM((chunk, width), F32)]
 
 
-def backward_carry(side, h, dy, whole):
+def backward_carry(side, h, dy, whole, number):
     (tokens, width), hidden, chunks = h.shape, whole[0].shape[1], side
+    chunk = hidden // chunks
     tok, col, row = blocks_of(h, whole[0], chunks)
-    dh, *terms = pl.pallas_call(
-        functools.partial(carry_kernel, chunks),
+    shapes = [(w.shape[0] // side**2, w.shape[1]) for w in whole]
+    one = pl.BlockSpec((width, chunk), lambda c: (0, 0))
+    copies = Scattering.copies(side, chunks)
+    summed = (shapes[0][0], hidden - chunk)
+    dh, gg, gu, gd, eg, eu = pl.pallas_call(
+        functools.partial(carry_kernel, side, chunks, shapes),
         grid=(chunks,),
         in_specs=[tok, tok, col, col, row],
-        out_specs=[tok, col, col, row],
-        out_shape=[jax.ShapeDtypeStruct(h.shape, BF)] + [jax.ShapeDtypeStruct(w.shape, BF) for w in whole],
-        scratch_shapes=[pltpu.VMEM((tokens, width), BF), *sums_of(whole[0], whole[2], chunks), pltpu.VMEM((tokens, width), F32)],
-        compiler_params=pltpu.CompilerParams(dimension_semantics=("arbitrary",), vmem_limit_bytes=VMEM_LIMIT),
+        out_specs=[tok, one, one, row, VMEM, VMEM],
+        out_shape=[
+            jax.ShapeDtypeStruct(h.shape, BF),
+            *[jax.ShapeDtypeStruct((width, chunk), BF)] * 2,
+            jax.ShapeDtypeStruct(whole[2].shape, BF),
+            *[jax.ShapeDtypeStruct(summed, BF)] * 2,
+        ],
+        scratch_shapes=[
+            pltpu.VMEM((tokens, width), BF),
+            *sums_of(whole[0], whole[2], chunks),
+            pltpu.VMEM((tokens, width), F32),
+            *(pltpu.VMEM((side, side, *s), BF) for s in shapes[:2]),
+            DMA((copies,)),
+            DMA((copies,)),
+            *Scattering.scratch(side, shapes),
+        ],
+        compiler_params=pltpu.CompilerParams(
+            dimension_semantics=("arbitrary",), vmem_limit_bytes=VMEM_LIMIT, collective_id=number, has_side_effects=True
+        ),
         cost_estimate=pl.CostEstimate(flops=16 * tokens * width * hidden, bytes_accessed=6 * tokens * width, transcendentals=tokens * hidden),
         name="backward_carry",
     )(h, dy, *whole)
-    return dh, terms
-
-
-def last_kernel(side, chunks, h_ref, dy_ref, wg_ref, wu_ref, wd_ref, *rest):
+    return dh, (gg, gu, gd), (eg, eu)
+
+
+def last_kernel(side, chunks, shapes, late, h_ref, dy_ref, wg_ref, wu_ref, wd_ref, *rest):
     later, outs, outs_later, (a_ref, sg, su, sd), mine, (send_sems, recv_sems), scratch = (
         rest[0:3], rest[3:6], rest[6:9], rest[9:13], rest[13:16], rest[16:18], rest[18:]
     )
     half = len(scratch) // 2
     c = pl.program_id(0)
     place = Place(side, send_sems, recv_sems)
-    above = Scattering(place, later, outs_later, scratch[:half], 1, 0, False)
-    here = Scattering(place, mine, outs, scratch[half:], chunks, Scattering.copies(side, 1), True)
+    above = Scattering(place, later, outs_later, scratch[:half], 1, 0, False, late)
+    here = Scattering(place, mine, outs, scratch[half:], chunks, Scattering.copies(side, 1), True, shapes)
     parts = range(4)
 
     @pl.when(c == 0)
@@ -501,22 +553,23 @@
 def backward_last(side, h, dy, whole, later, number):
     (tokens, width), hidden, chunks = h.shape, whole[0].shape[1], side
     tok, col, row = blocks_of(h, whole[0], chunks)
-    shapes = [(t.shape[0] // side**2, t.shape[1]) for t in later]
+    late = [(t.shape[0] // side**2, t.shape[1]) for t in later]
+    shapes = [(w.shape[0] // side**2, w.shape[1]) for w in whole]
     views = [(side, side, *s) for s in shapes]
     copies = Scattering.copies(side, 1) + Scattering.copies(side, chunks)
     found = pl.pallas_call(
-        functools.partial(last_kernel, side, chunks),
+        functools.partial(last_kernel, side, chunks, shapes, late),
         grid=(chunks,),
         in_specs=[tok, tok, col, col, row] + [HBM] * 3,
         out_specs=[VMEM] * 6,
-        out_shape=[jax.ShapeDtypeStruct(s, BF) for s in shapes + shapes],
+        out_shape=[jax.ShapeDtypeStruct(s, BF) for s in shapes + late],
         scratch_shapes=[
             pltpu.VMEM((tokens, width), BF),
             *sums_of(whole[0], whole[2], chunks),
             *(pltpu.VMEM(v, BF) for v in views),
             DMA((copies,)),
             DMA((copies,)),
-            *Scattering.scratch(side, shapes),
+            *Scattering.scratch(side, late),
             *Scattering.scratch(side, shapes),
         ],
         compiler_params=pltpu.CompilerParams(
@@ -524,7 +577,7 @@
         ),
         cost_estimate=pl.CostEstimate(flops=12 * tokens * width * hidden, bytes_accessed=4 * tokens * width, transcendentals=tokens * hidden),
         name="backward_last",
-    )(h, dy, *whole, *(t.reshape(v) for t, v in zip(later, views, strict=True)))
+    )(h, dy, *whole, *(t.reshape(side, side, *s) for t, s in zip(later, late, strict=True)))
     return found[:3], found[3:]
 
 
@@ -545,8 +598,9 @@
         low = flat(gather(side, 0, weights[:2], 1))
         above, down, high = forward(side, h, low, weights, 1, 2)
         low += flat([down])
-        dh, terms = backward_carry(side, above, dy[0], flat(high))
-        mine = backward_last(side, h, dh, low, terms, 3)
+        dh, terms, early = backward_carry(side, above, dy[0], flat(high), 4)
+        first, second = backward_last(side, h, dh, low, terms, 3)
+        mine = [first, [jnp.concatenate(pair, 1) for pair in zip(early, second[:2], strict=True)] + [second[2]]]
         gradients = [jnp.stack([mine[number][i] for number in range(2)]).astype(F32) for i in range(3)]
         new = [adamw(w.astype(F32), m, v, g) for w, m, v, g in zip(weights, m, v, gradients, strict=True)]
         return tuple(one[which] for which in range(3) for one in new)

time: 294 us -> 289 us (0.983)
  Pallas kernels: 285 us -> 280 us
    pallas_call x1, Pallas kernels: 54.3 us -> 49.1 us  [forward(): pl.pallas_call(functools.partial(forward_kernel, side, chunks, layer), gr...]
where the time goes in v4:
time: 289 us; the launch traced here: 287 us
  Pallas kernels  280 us (97%)
  other arithmetic  5.57 us (2%)
    pallas_call x1, Pallas kernels, backward_carry(): pl.pallas_call(functools.partial(carry_kernel, side, chunks, shapes), gri...  104 us
    pallas_call x1, Pallas kernels, backward_last(): pl.pallas_call(functools.partial(last_kernel, side, chunks, shapes, late)...  98 us
    pallas_call x1, Pallas kernels, forward(): pl.pallas_call(functools.partial(forward_kernel, side, chunks, layer), gr...  49.1 us
    pallas_call x1, Pallas kernels, gather(): pl.pallas_call(functools.partial(gather_kernel, side, layer), in_specs=[V...  29.1 us

profile of v4, /device:TPU:97, one launch (start us, length us, event | category | flops | bytes accessed | tf_op | source)
XLA Modules:
  0.0 286.9 jit_solution(13976229004789001418)
XLA Ops:
  0.6 29.1 %gather_1.1 = (bf16[4,4,32,2048]{3,2,1,0:T(8,128)(2,1)}, bf16[4,4,32,2048]{3,2,1,0:T(8,128)(2,1)}) custom-call(bf16[2,32,2048]{2,1,0:T(8,128)(2,1)} %g.3, bf16[2,32,2048]{2,1,0:T(8,128)(2,1)} %u.3), custom_call_target="tpu_custom_call" | custom-call | tf_op jit(solution)/shard_map/gather_1/pallas_call | solution.py:147
  29.8 49.1 %forward.1 = (bf16[4096,512]{1,0:T(8,128)(2,1)}, bf16[4,4,128,512]{3,2,1,0:T(8,128)(2,1)}, bf16[4,4,32,2048]{3,2,1,0:T(8,128)(2,1)}, bf16[4,4,32,2048]{3,2,1,0:T(8,128)(2,1)}, bf16[4,4,128,512]{3,2,1,0:T(8,128)(2,1)}) custom-call(bf16[4096,512]{1,0:T(8,128)(2,1)} %bitcast.24, bf16[512,2048]{1,0:T(8,128)(2,1)} %bitcast.26, bf16[512,2048]{1,0:T(8,128)(2,1)} %bitcast.28, ...), custom_call_target="tpu_custom_call" | custom-call | flops 25769803776 | bytes 8388608 | tf_op jit(solution)/shard_map/forward/pallas_call | solution.py:367
  78.9 103.7 %backward_carry.1 = (bf16[4096,512]{1,0:T(8,128)(2,1)}, bf16[512,512]{1,0:T(8,128)(2,1)}, bf16[512,512]{1,0:T(8,128)(2,1)}, bf16[2048,512]{1,0:T(8,128)(2,1)}, b...) custom-call(bf16[4096,512]{1,0:T(8,128)(2,1)} %get-tuple-element.30.h_ref, bf16[4096,512]{1,0:T(8,128)(2,1)} %bitcast.23, ...), custom_call_target="tpu_custom_call" | custom-call | flops 68719476736 | bytes 12582912 | tf_op jit(solution)/shard_map/backward_carry/pallas_call | solution.py:476
  182.6 0.0 copy-start.11
  182.6 0.0 copy-start.12
  182.6 0.0 copy-start
  182.6 0.0 copy-start.2
  182.7 98.0 %backward_last.1 = (bf16[32,2048]{1,0:T(8,128)(2,1)}, bf16[32,2048]{1,0:T(8,128)(2,1)}, bf16[128,512]{1,0:T(8,128)(2,1)}, bf16[32,512]{1,0:T(8,128)(2,1)}, bf16[...) custom-call(bf16[4096,512]{1,0:T(8,128)(2,1)} %bitcast.25, bf16[4096,512]{1,0:T(8,128)(2,1)} %get-tuple-element.34.dy_ref, ...), custom_call_target="tpu_custom_call" | custom-call | flops 51539607552 | bytes 8388608 | tf_op jit(solution)/shard_map/backward_last/pallas_call | solution.py:560
  280.6 0.0 copy-start.1
  280.7 0.0 copy-start.3
  280.7 0.0 copy-start.4
  280.7 0.0 copy-start.10
  280.7 0.0 copy-done.11
  280.7 0.0 copy-done.12
  280.7 0.9 maximum_bitcast_fusion
  281.6 0.0 copy-done
  281.6 0.0 copy-done.2
  281.6 2.3 fusion.2
  283.9 0.0 copy-start.5
  283.9 0.0 copy-start.6
  283.9 0.0 copy-start.7
  283.9 0.0 copy-start.8
  283.9 0.0 copy-start.9
  283.9 0.0 copy-done.1
  284.0 0.0 copy-done.3
  284.0 0.0 copy-done.4
  284.0 0.0 copy-done.10
  284.0 1.2 fusion.6
  285.2 0.0 copy-done.5
  285.2 0.3 copy-done.6
  285.4 0.2 copy-done.7
  285.7 0.0 copy-done.8
  285.7 0.0 copy-done.9
  285.7 1.2 fusion.10
Async XLA Ops:
  182.6 98.1 %copy-start.11 = (bf16[32,1536]{1,0:T(8,128)(2,1)S(1)}, bf16[32,1536]{1,0:T(8,128)(2,1)}, u32[]{:S(2)}) copy-start(bf16[32,1536]{1,0:T(8,128)(2,1)} %get-tuple-element.40) | copy-start | bytes 294916
  182.6 98.1 %copy-start.12 = (bf16[32,1536]{1,0:T(8,128)(2,1)S(1)}, bf16[32,1536]{1,0:T(8,128)(2,1)}, u32[]{:S(2)}) copy-start(bf16[32,1536]{1,0:T(8,128)(2,1)} %get-tuple-element.43) | copy-start | bytes 294916
  182.6 99.0 %copy-start = (bf16[2,32,2048]{2,1,0:T(8,128)(2,1)S(1)}, bf16[2,32,2048]{2,1,0:T(8,128)(2,1)}, u32[]{:S(2)}) copy-start(bf16[2,32,2048]{2,1,0:T(8,128)(2,1)} %g.3) | copy-start | bytes 786436
  182.6 99.0 %copy-start.2 = (f32[2,32,2048]{2,1,0:T(8,128)S(1)}, f32[2,32,2048]{2,1,0:T(8,128)}, u32[]{:S(2)}) copy-start(f32[2,32,2048]{2,1,0:T(8,128)} %param.19) | copy-start | bytes 1572868
  280.6 3.3 %copy-start.1 = (bf16[2,32,2048]{2,1,0:T(8,128)(2,1)S(1)}, bf16[2,32,2048]{2,1,0:T(8,128)(2,1)}, u32[]{:S(2)}) copy-start(bf16[2,32,2048]{2,1,0:T(8,128)(2,1)} %u.3) | copy-start | bytes 786436
  280.7 3.3 %copy-start.3 = (f32[2,32,2048]{2,1,0:T(8,128)S(1)}, f32[2,32,2048]{2,1,0:T(8,128)}, u32[]{:S(2)}) copy-start(f32[2,32,2048]{2,1,0:T(8,128)} %param.20) | copy-start | bytes 1572868
  280.7 3.3 %copy-start.4 = (f32[2,32,2048]{2,1,0:T(8,128)S(1)}, f32[2,32,2048]{2,1,0:T(8,128)}, u32[]{:S(2)}) copy-start(f32[2,32,2048]{2,1,0:T(8,128)} %param.17) | copy-start | bytes 1572868
  280.7 3.3 %copy-start.10 = (bf16[32,2048]{1,0:T(8,128)(2,1)S(1)}, bf16[32,2048]{1,0:T(8,128)(2,1)}, u32[]{:S(2)}) copy-start(bf16[32,2048]{1,0:T(8,128)(2,1)} %get-tuple-element.42) | copy-start | bytes 393220
  283.9 1.2 copy-start.5
  283.9 1.5 copy-start.6
  283.9 1.7 copy-start.7
  283.9 1.8 copy-start.8
  283.9 1.8 copy-start.9
